TPU v7x, 32 devices: a whole 2x2x4 slice. The times are simulated.
32 devices in a mesh: region: 2 (over y), super: 16 (over z, x, core).
Axes of the slice: x: 2, y: 2, z: 4, core: 2. Of those that a mesh axis runs over, the one named last changes fastest.
Arguments:
- obs_coords: float32 [2, 131072], P(None, ('region', 'super')), may hold values from 0 to 1, as said below
- obs_values: bfloat16 [64, 131072], P(None, ('region', 'super')), may hold values from -6 to 6
- obs_precision: float32 [131072], P(('region', 'super')), may hold values from 0.0009765625 to 0.009765625
- site_coords: float32 [2, 16384], P(None, ('region', 'super')), may hold values from 0 to 1, as said below
- length_scale: float32 [3], replicated, may hold values from 0.009375 to 0.3, as said below
- global_knots: float32 [2, 256], replicated, may hold values from 0 to 1
- region_knots: float32 [16, 2, 256], P('super'), may hold values from 0 to 1, as said below
- leaf_knots: float32 [32, 2, 256], P(('region', 'super')), may hold values from 0 to 1, as said below
- global_prior: float32 [256, 256], replicated, as said below
- region_prior: float32 [16, 256, 256], P('super'), as said below
- leaf_prior: float32 [32, 256, 256], P(('region', 'super')), as said below
Outputs:
- prediction: float32 [64, 16384], P(None, ('region', 'super'))
Inputs may be any that keep to these rules, and one draw needn't show every extreme that they name: `global_prior`: symmetric; each diagonal entry exceeds the sum of magnitudes of the other entries of its row. `region_prior`: each region's matrix symmetric; each diagonal entry exceeds the sum of magnitudes of the other entries of its row. `leaf_prior`: each leaf's matrix symmetric; each diagonal entry exceeds the sum of magnitudes of the other entries of its row. `obs_coords`: the region cells tile the unit square as a grid, each split into a grid of leaf cells; leaf l's observations lie inside leaf l's cell. `site_coords`: leaf l's sites lie inside leaf l's cell. `region_knots`: region g's knots lie inside region g's cell. `leaf_knots`: leaf l's knots lie inside leaf l's cell. `length_scale`: the global scale lies in 0.15 to 0.3, the regional scale in 0.7 to 1.0 times 1 / sqrt(4096), the leaf scale in 0.3 to 0.9 times 1 / sqrt(32).
All inputs are finite; a program needn't handle non-finite values.
Results may differ from a plain program's by a relative error of at most 0.0003.
The roundings to bfloat16 on the way count: a program that leaves them out, or rounds other values in their place, can miss the bound.
Values sent between devices are 32-bit elements; how exact they have to be, the bound alone decides.
No kernel may reach another device: no remote copies, remote signals or barrier semaphores. Data moves between devices by JAX's collectives and lax.ppermute only.
A program may use at most 64 MiB of HBM per device.

v0:
```python
import jax
import jax.numpy as jnp
from jax import lax
from jax.sharding import PartitionSpec as P

R = 256


HIGH = lax.Precision.HIGHEST


def basis_rows(coords, knots, scale):
    diff_x = coords[0][:, None] - knots[0][None, :]
    diff_y = coords[1][:, None] - knots[1][None, :]
    return jnp.exp(-0.5 * (diff_x * diff_x + diff_y * diff_y) / (scale * scale))


def basis_cols(knots, coords, scale):
    diff_x = knots[0][:, None] - coords[0][None, :]
    diff_y = knots[1][:, None] - coords[1][None, :]
    return jnp.exp(-0.5 * (diff_x * diff_x + diff_y * diff_y) / (scale * scale))


def leaf_terms(coords, values, precision, knots_g, knots_r, knots_l, scales, prior_l):
    weight = jnp.sqrt(precision)[:, None]
    stacked = jnp.concatenate(
        [
            basis_rows(coords, knots_g, scales[0]),
            basis_rows(coords, knots_r, scales[1]),
            basis_rows(coords, knots_l, scales[2]),
            values.astype(jnp.float32).T,
        ],
        axis=1,
    )
    scaled = (stacked * weight).astype(jnp.bfloat16)
    gram = lax.dot_general(
        scaled, scaled, (((0,), (0,)), ((), ())), preferred_element_type=jnp.float32
    )
    cross = gram[2 * R : 3 * R, : 2 * R]
    factor = jnp.linalg.cholesky(prior_l + gram[2 * R : 3 * R, 2 * R : 3 * R])
    rhs = jnp.concatenate([cross, gram[2 * R : 3 * R, 3 * R :]], axis=1)
    solved = jax.scipy.linalg.cho_solve((factor, True), rhs)
    left = jnp.concatenate([gram[: 2 * R, : 2 * R], gram[: 2 * R, 3 * R :]], axis=1)
    schur = left - jnp.dot(cross.T, solved, precision=HIGH)
    return (schur, solved)


def region_terms(rows, prior_r):
    factor = jnp.linalg.cholesky(prior_r + rows[:, R : 2 * R])
    rhs = jnp.concatenate([rows[:, :R], rows[:, 2 * R :]], axis=1)
    solved = jax.scipy.linalg.cho_solve((factor, True), rhs)
    correction = jnp.dot(rows[:, :R].T, solved, precision=HIGH)
    return (solved, correction)


def global_part(schur):
    return jnp.concatenate([schur[:R, :R], schur[:R, 2 * R :]], axis=1)


def shards(
    obs_coords,
    obs_values,
    obs_precision,
    site_coords,
    length_scale,
    global_knots,
    region_knots,
    leaf_knots,
    global_prior,
    region_prior,
    leaf_prior,
):
    schur, solved = leaf_terms(
        obs_coords,
        obs_values,
        obs_precision,
        global_knots,
        region_knots[0],
        leaf_knots[0],
        length_scale,
        leaf_prior[0],
    )
    summed = lax.psum(schur, "region")
    region_solved, correction = region_terms(summed[R : 2 * R], region_prior[0])
    upper = lax.psum(global_part(summed) - correction, "super")
    factor = jnp.linalg.cholesky(global_prior + upper[:, :R])
    global_weights = jax.scipy.linalg.cho_solve((factor, True), upper[:, R:])
    region_weights = region_solved[:, R:] - jnp.dot(
        region_solved[:, :R], global_weights, precision=HIGH
    )
    upper_weights = jnp.concatenate([global_weights, region_weights], axis=0)
    leaf_weights = solved[:, 2 * R :] - jnp.dot(solved[:, : 2 * R], upper_weights, precision=HIGH)
    weights = jnp.concatenate([upper_weights, leaf_weights], axis=0)
    table = jnp.concatenate(
        [
            basis_cols(global_knots, site_coords, length_scale[0]),
            basis_cols(region_knots[0], site_coords, length_scale[1]),
            basis_cols(leaf_knots[0], site_coords, length_scale[2]),
        ],
        axis=0,
    )
    return jnp.dot(weights.T, table, precision=HIGH)


def solution(mesh):
    in_specs = (
        P(None, ("region", "super")),
        P(None, ("region", "super")),
        P(("region", "super")),
        P(None, ("region", "super")),
        P(),
        P(),
        P("super", None, None),
        P(("region", "super"), None, None),
        P(),
        P("super", None, None),
        P(("region", "super"), None, None),
    )
    out_specs = P(None, ("region", "super"))
    return jax.shard_map(shards, mesh=mesh, in_specs=in_specs, out_specs=out_specs, check_vma=False)
```

profile of v0, /device:TPU:0, one launch (start us, length us, event | category | flops | bytes accessed | tf_op | source)
XLA Modules:
  0.0 374.1 jit_solution(8886739177236832170)
XLA Ops:
  6.5 1.4 fusion.99
  14.9 1.1 convert_bitcast_fusion
  16.7 4.0 %divide_exponential_fusion.2 = (f32[4096,256]{1,0:T(8,128)S(1)}, f32[4096,256]{1,0:T(8,128)S(1)}, f32[4096,256]{1,0:T(8,128)S(1)}) fusion(f32[]{:T(128)} %bitcast.4, f32[256]{0:T(256)S(1)} %bitcast.131, f32[4096]{0:T(1024)S(1)} %bitcast.128, f32[256]{0:T(256)S(1)} %bitcast.129, f32[4096]{0:T(1024)S(1)} %bitcast.127, f32[]{:T(128)} %bitcast.7, ...), kind=kLoop, calls=%fused_computation.11 | loop fusion | flops 22020096 | bytes 12621836 | tf_op jit(solution)/shard_map/exp | solution.py:15
  20.7 8.0 %fusion.1 = f32[832,832]{0,1:T(8,128)S(1)} fusion(f32[4096,64]{1,0:T(8,128)S(1)} %copy.12, f32[4096,256]{1,0:T(8,128)S(1)} %get-tuple-element.79, f32[4096,256]{1,0:T(8,128)S(1)} %get-tuple-element.78, f32[4096,256]{1,0:T(8,128)S(1)} %get-tuple-element.77, f32[4096]{0:T(1024)S(1)} %sqrt.3), kind=kOutput, calls=%fused_computation.8 | convolution fusion | flops 5687738368 | bytes 16416768 | tf_op jit(solution)/shard_map/dot_general | solution.py:36
  28.9 1.4 copy-done
  31.7 11.7 %cholesky.172 = f32[128,128]{1,0:T(8,128)S(1)} custom-call(f32[128,128]{1,0:T(8,128)S(1)} %cholesky.270), custom_call_target="Cholesky" | custom-call | tf_op jit(solution)/shard_map/jit(cholesky)/cholesky | solution.py:40
  43.4 10.2 %custom-call.34 = f32[1,128,128]{1,2,0:T(8,128)S(1)} custom-call(f32[1,128,128]{2,1,0:T(8,128)S(1)} %get-tuple-element.76), custom_call_target="InvertDiagBlocksLowerTriangular" | custom-call | tf_op jit(solution)/shard_map/jit(cholesky)/cholesky | solution.py:40
  54.1 11.7 %cholesky.189 = f32[128,128]{1,0:T(8,128)S(1)} custom-call(f32[128,128]{1,0:T(8,128)S(1)} %convolution_subtract_fusion.9), custom_call_target="Cholesky" | custom-call | tf_op jit(solution)/shard_map/jit(cholesky)/cholesky | solution.py:40
  67.9 3.9 %while.3 = (s32[]{:T(128)}, f32[256,256]{1,0:T(8,128)S(1)}, s32[2,2]{1,0:T(2,128)S(1)}, f32[2,128,128]{2,1,0:T(8,128)S(1)}, s32[]{:T(128)}) while((s32[]{:T(128)}, f32[256,256]{1,0:T(8,128)S(1)}, s32[2,2]{1,0:T(2,128)S(1)}, f32[2,128,128]{2,1,0:T(8,128)S(1)}, s32[]{:T(128)}) %tuple.72), condition=%wide.while_cond, body=%wide.while_body.sunk | while | flops 2 | bytes 131181 | solution.py:42
  68.6 1.3 bitcast_dynamic-update-slice_fusion.6
  70.5 1.3 bitcast_dynamic-update-slice_fusion.6
  71.9 19.7 %custom-call.29 = f32[2,128,128]{1,2,0:T(8,128)S(1)} custom-call(f32[2,128,128]{2,1,0:T(8,128)S(1)} %get-tuple-element.13), custom_call_target="InvertDiagBlocksLowerTriangular" | custom-call | tf_op jit(solution)/shard_map/jit(_cho_solve)/triangular_solve | solution.py:42
  94.4 3.2 convolution_subtract_fusion
  98.2 45.3 %all-reduce.4.cloned.1.call-done = f32[512,576]{0,1:T(8,128)} async-done(((f32[512,576]{0,1:T(8,128)}), f32[512,576]{0,1:T(8,128)}) %all-reduce.4.cloned.1.call-update) | async-done | bytes 1179664 | tf_op jit(solution)/shard_map/psum | solution.py:83
  143.5 1.2 fusion.92
  144.8 11.7 %cholesky.206 = f32[128,128]{1,0:T(8,128)S(1)} custom-call(f32[128,128]{1,0:T(8,128)S(1)} %cholesky.273), custom_call_target="Cholesky" | custom-call | tf_op jit(solution)/shard_map/jit(cholesky)/cholesky | solution.py:49
  156.6 9.8 %custom-call.35 = f32[1,128,128]{1,2,0:T(8,128)S(1)} custom-call(f32[1,128,128]{2,1,0:T(8,128)S(1)} %get-tuple-element.72), custom_call_target="InvertDiagBlocksLowerTriangular" | custom-call | tf_op jit(solution)/shard_map/jit(cholesky)/cholesky | solution.py:49
  166.9 11.7 %cholesky.223 = f32[128,128]{1,0:T(8,128)S(1)} custom-call(f32[128,128]{1,0:T(8,128)S(1)} %convolution_subtract_fusion.8), custom_call_target="Cholesky" | custom-call | tf_op jit(solution)/shard_map/jit(cholesky)/cholesky | solution.py:49
  181.3 3.9 %while.4 = (s32[]{:T(128)}, f32[256,256]{1,0:T(8,128)S(1)}, s32[2,2]{1,0:T(2,128)S(1)}, f32[2,128,128]{2,1,0:T(8,128)S(1)}, s32[]{:T(128)}) while((s32[]{:T(128)}, f32[256,256]{1,0:T(8,128)S(1)}, s32[2,2]{1,0:T(2,128)S(1)}, f32[2,128,128]{2,1,0:T(8,128)S(1)}, s32[]{:T(128)}) %tuple.85), condition=%wide.while_cond.1, body=%wide.while_body.1.sunk | while | flops 2 | bytes 131181 | solution.py:51
  181.9 1.3 bitcast_dynamic-update-slice_fusion.7
  183.8 1.3 bitcast_dynamic-update-slice_fusion.7
  185.2 19.9 %custom-call.30 = f32[2,128,128]{1,2,0:T(8,128)S(1)} custom-call(f32[2,128,128]{2,1,0:T(8,128)S(1)} %get-tuple-element.21), custom_call_target="InvertDiagBlocksLowerTriangular" | custom-call | tf_op jit(solution)/shard_map/jit(_cho_solve)/triangular_solve | solution.py:51
  208.1 2.2 convolution_subtract_fusion.1
  210.8 89.0 %all-reduce.6.cloned.1.call-done = f32[256,320]{0,1:T(8,128)} async-done(((f32[256,320]{0,1:T(8,128)}), f32[256,320]{0,1:T(8,128)}) %all-reduce.6.cloned.1.call-update) | async-done | bytes 327696 | tf_op jit(solution)/shard_map/psum | solution.py:85
  301.0 11.7 %cholesky.240 = f32[128,128]{1,0:T(8,128)S(1)} custom-call(f32[128,128]{1,0:T(8,128)S(1)} %cholesky.276), custom_call_target="Cholesky" | custom-call | tf_op jit(solution)/shard_map/jit(cholesky)/cholesky | solution.py:86
  312.8 9.8 %custom-call.36 = f32[1,128,128]{1,2,0:T(8,128)S(1)} custom-call(f32[1,128,128]{2,1,0:T(8,128)S(1)} %get-tuple-element.68), custom_call_target="InvertDiagBlocksLowerTriangular" | custom-call | tf_op jit(solution)/shard_map/jit(cholesky)/cholesky | solution.py:86
  323.1 11.9 %cholesky.257 = f32[128,128]{1,0:T(8,128)S(1)} custom-call(f32[128,128]{1,0:T(8,128)S(1)} %convolution_subtract_fusion.7), custom_call_target="Cholesky" | custom-call | tf_op jit(solution)/shard_map/jit(cholesky)/cholesky | solution.py:86
  337.8 4.1 %while.5 = (s32[]{:T(128)}, f32[256,256]{1,0:T(8,128)S(1)}, s32[2,2]{1,0:T(2,128)S(1)}, f32[2,128,128]{2,1,0:T(8,128)S(1)}, s32[]{:T(128)}) while((s32[]{:T(128)}, f32[256,256]{1,0:T(8,128)S(1)}, s32[2,2]{1,0:T(2,128)S(1)}, f32[2,128,128]{2,1,0:T(8,128)S(1)}, s32[]{:T(128)}) %tuple.86), condition=%wide.while_cond.2, body=%wide.while_body.2.sunk | while | flops 2 | bytes 131181 | solution.py:87
  338.4 1.4 bitcast_dynamic-update-slice_fusion.8
  340.5 1.4 bitcast_dynamic-update-slice_fusion.8
  341.9 19.7 %custom-call.31 = f32[2,128,128]{1,2,0:T(8,128)S(1)} custom-call(f32[2,128,128]{2,1,0:T(8,128)S(1)} %get-tuple-element.29), custom_call_target="InvertDiagBlocksLowerTriangular" | custom-call | tf_op jit(solution)/shard_map/jit(_cho_solve)/triangular_solve | solution.py:87
  365.3 1.7 fusion.3
  (102 shorter events, 25.9 us)
Async XLA Ops:
  6.5 10.1 %copy-start.4 = (f32[4096]{0:T(1024)S(1)}, f32[4096]{0:T(1024)}, u32[]{:S(2)}) copy-start(f32[4096]{0:T(1024)} %param.14) | copy-start | bytes 49156
  6.5 136.9 %all-reduce.4.cloned.1.call-start = ((), (), s32[]{:S(2)}) async-start(), calls=%async_computation | async-start | bytes 2359296 | tf_op jit(solution)/shard_map/psum | solution.py:83
  20.7 9.7 %copy-start.1 = (f32[1,256,256]{2,1,0:T(8,128)S(1)}, f32[1,256,256]{2,1,0:T(8,128)}, u32[]{:S(2)}) copy-start(f32[1,256,256]{2,1,0:T(8,128)} %param.22) | copy-start | bytes 786436
  28.7 1.6 copy-start
  91.9 5.9 %copy-start.2 = (f32[1,256,256]{2,1,0:T(8,128)S(1)}, f32[1,256,256]{2,1,0:T(8,128)}, u32[]{:S(2)}) copy-start(f32[1,256,256]{2,1,0:T(8,128)} %param.21) | copy-start | bytes 786436
  92.4 5.7 %copy-start.3 = (f32[256,256]{1,0:T(8,128)S(1)}, f32[256,256]{1,0:T(8,128)}, u32[]{:S(2)}) copy-start(f32[256,256]{1,0:T(8,128)} %param.20) | copy-start | bytes 786436
  92.4 5.8 %copy-start.5 = (f32[2,512]{1,0:T(2,128)S(1)}, f32[2,512]{1,0:T(2,128)}, u32[]{:S(2)}) copy-start(f32[2,512]{1,0:T(2,128)} %param.15) | copy-start | bytes 12292
  97.6 202.2 %all-reduce.6.cloned.1.call-start = ((), (), s32[]{:S(2)}) async-start(), calls=%async_computation.1 | async-start | bytes 655360 | tf_op jit(solution)/shard_map/psum | solution.py:85
Sparse Core Ops, SparseCore 0:
  97.8 45.6 all-reduce.3
  210.4 89.3 all-reduce.5
where the time goes:
time: 378 us; the launch traced here: 374 us
  other arithmetic  172 us (46%)
  waiting for transfers between devices  134 us (35%)
  matrix products  25 us (7%)
  between operations  21.9 us (6%)
  local copies, waits for them, and re-layouts  20.4 us (5%)
    psum x1, waiting for transfers between devices, shards(): upper = lax.psum(global_part(summed) - correction, 'super')  89 us
    psum x1, waiting for transfers between devices, shards(): summed = lax.psum(schur, 'region')  45.3 us
    another operation x7, other arithmetic, shards(): factor = jnp.linalg.cholesky(global_prior + upper[:, :R])  34.9 us
    another operation x7, other arithmetic, region_terms(): factor = jnp.linalg.cholesky(prior_r + rows[:, R:2 * R])  34.6 us
    another operation x6, other arithmetic, leaf_terms(): factor = jnp.linalg.cholesky(prior_l + gram[2 * R:3 * R, 2 * R:3 * R])  34.4 us
    another operation x2, other arithmetic, region_terms(): solved = jax.scipy.linalg.cho_solve((factor, True), rhs)  19.9 us
    another operation x3, other arithmetic, leaf_terms(): solved = jax.scipy.linalg.cho_solve((factor, True), rhs)  19.7 us
    another operation x2, other arithmetic, shards(): global_weights = jax.scipy.linalg.cho_solve((factor, True), upper[:, R:])  19.7 us
  transfers between devices with their start and end apart: 2, of which 2 were waited for; matrix products, arithmetic and copies ran while one was open for 0% of the time, Pallas kernels for 0%

commit v1 on v0

v1 whole, which is shorter than its diff:
```python
import functools

import jax
import jax.numpy as jnp
from jax import lax
from jax.experimental import pallas as pl
from jax.experimental.pallas import tpu as pltpu
from jax.sharding import PartitionSpec as P

HIGH = lax.Precision.HIGHEST
F32 = jnp.float32


def mm(a, b, ca=1, cb=0):
    return lax.dot_general(a, b, (((ca,), (cb,)), ((), ())), precision=HIGH, preferred_element_type=F32)


def spd_inverse(a):
    n = a.shape[0]
    groups = n // 8
    rows = [a[8 * i : 8 * i + 8, :] for i in range(groups)]
    lane = lax.broadcasted_iota(jnp.int32, (8, n), 1)
    sub = lax.broadcasted_iota(jnp.int32, (8, n), 0)
    for g in range(groups):

        def col(x, k, g=g):
            return jnp.broadcast_to(x[:, 8 * g + k : 8 * g + k + 1], (8, n))

        p = rows[g]
        c = [col(p, k) for k in range(8)]
        inside = (lane >= 8 * g) & (lane < 8 * g + 8)
        p = jnp.where(inside, jnp.where(lane - 8 * g == sub, 1.0, 0.0), p)
        for k in range(8):
            here = sub == k
            r = 1.0 / jnp.broadcast_to(c[k][k : k + 1, :], (8, n))
            for m in range(k + 1, 8):
                s = jnp.broadcast_to(c[m][k : k + 1, :], (8, n)) * r
                c[m] = jnp.where(here, s, c[m] - c[k] * s)
            s = jnp.broadcast_to(p[k : k + 1, :], (8, n)) * r
            p = jnp.where(here, s, p - c[k] * s)
        pr = [jnp.broadcast_to(p[k : k + 1, :], (8, n)) for k in range(8)]
        for i in range(groups):
            if i == g:
                continue
            old = rows[i]
            t = [col(old, k) * pr[k] for k in range(8)]
            while len(t) > 1:
                t = [t[q] + t[q + 1] for q in range(0, len(t), 2)]
            rows[i] = jnp.where(inside, 0.0, old) - t[0]
        rows[g] = p
    return jnp.concatenate(rows, axis=0)


def spd_solve(a, b):
    h = a.shape[0] // 2
    a12 = a[:h, h:]
    i1 = spd_inverse(a[:h, :h])
    t = mm(i1, a12)
    i2 = spd_inverse(a[h:, h:] - mm(a12, t, 0, 0))
    x2 = mm(i2, b[h:] - mm(t, b[:h], 0, 0))
    x1 = mm(i1, b[:h]) - mm(t, x2)
    return jnp.concatenate([x1, x2], axis=0)


def leaf_kernel(chunks, scale_ref, knots_ref, coords_ref, values_ref, prec_ref, prior_ref,
                rows_ref, upper_ref, solved_ref, za, zb, acc_g, acc_r, acc_v):
    r = prior_ref.shape[0]
    width = za.shape[1]

    def fill(z, chunk):
        cols = pl.ds(pl.multiple_of(chunk * width, width), width)
        px = coords_ref[0:1, cols]
        py = coords_ref[1:2, cols]
        weight = jnp.sqrt(prec_ref[0:1, cols])
        for level in range(3):
            factor = -0.5 / (scale_ref[level] * scale_ref[level])
            dx = knots_ref[level * r : (level + 1) * r, 0:1] - px
            dy = knots_ref[level * r : (level + 1) * r, 1:2] - py
            basis = jnp.exp((dx * dx + dy * dy) * factor)
            z[level * r : (level + 1) * r, :] = (basis * weight).astype(jnp.bfloat16)
        z[3 * r :, :] = (values_ref[:, cols].astype(F32) * weight).astype(jnp.bfloat16)

    def gram(z):
        for level, acc in enumerate((acc_g, acc_r, acc_v)):
            acc[...] += lax.dot_general(
                z[level * r :, :], z[level * r : (level + 1) * r, :], (((1,), (1,)), ((), ())),
                preferred_element_type=F32,
            )

    acc_g[...] = jnp.zeros_like(acc_g)
    acc_r[...] = jnp.zeros_like(acc_r)
    acc_v[...] = jnp.zeros_like(acc_v)
    fill(za, 0)

    def step(i, carry):
        fill(zb, 2 * i + 1)
        gram(za)
        fill(za, jnp.minimum(2 * i + 2, chunks - 1))
        gram(zb)
        return carry

    lax.fori_loop(0, chunks // 2, step, 0)
    y_cols = jnp.transpose(jnp.concatenate([acc_g[3 * r :, :], acc_r[2 * r :, :], acc_v[r:, :]], axis=1))
    cross_g = acc_g[2 * r : 3 * r, :]
    cross_r = acc_r[r : 2 * r, :]
    x = spd_solve(prior_ref[...] + acc_v[:r, :], jnp.concatenate([cross_g, cross_r, y_cols[2 * r :]], axis=1))
    solved_ref[...] = x
    left = jnp.concatenate([acc_g[r : 2 * r, :], acc_r[:r, :], y_cols[r : 2 * r]], axis=1)
    rows_ref[...] = left - mm(cross_r, x, 0, 0)
    left = jnp.concatenate([acc_g[:r, :], y_cols[:r]], axis=1)
    upper_ref[...] = left - mm(cross_g, jnp.concatenate([x[:, :r], x[:, 2 * r :]], axis=1), 0, 0)


def region_kernel(share, half_ref, own_ref, other_ref, prior_ref, upper_ref, solved_ref, keep_ref, send_ref, delta):
    r = prior_ref.shape[0]
    rows = own_ref[...] + other_ref[...]
    cross = rows[:, :r]
    x = spd_solve(prior_ref[...] + rows[:, r : 2 * r], jnp.concatenate([cross, rows[:, 2 * r :]], axis=1))
    solved_ref[...] = x
    delta[...] = upper_ref[...] - mm(cross, x, 0, 0) * share
    h = r // 2
    mine = half_ref[0] * h
    keep_ref[...] = delta[pl.ds(pl.multiple_of(mine, h), h), :]
    send_ref[...] = delta[pl.ds(pl.multiple_of(h - mine, h), h), :]


def global_kernel(half_ref, mine_ref, other_ref, prior_ref, region_ref, leaf_ref, table_ref, out_ref, upper):
    r = prior_ref.shape[0]
    h = r // 2
    mine = half_ref[0] * h
    upper[pl.ds(pl.multiple_of(mine, h), h), :] = mine_ref[...]
    upper[pl.ds(pl.multiple_of(h - mine, h), h), :] = other_ref[...]
    w_g = spd_solve(prior_ref[...] + upper[:, :r], upper[:, r:])
    w_r = region_ref[:, r:] - mm(region_ref[:, :r], w_g)
    w_l = leaf_ref[:, 2 * r :] - mm(leaf_ref[:, : 2 * r], jnp.concatenate([w_g, w_r], axis=0))
    out_ref[...] = mm(jnp.concatenate([w_g, w_r, w_l], axis=0), table_ref[...], 0, 0)


def basis_cols(knots, coords, scale):
    diff_x = knots[0][:, None] - coords[0][None, :]
    diff_y = knots[1][:, None] - coords[1][None, :]
    return jnp.exp(-0.5 * (diff_x * diff_x + diff_y * diff_y) / (scale * scale))


SMEM = pl.BlockSpec(memory_space=pltpu.SMEM)
VMEM = pl.BlockSpec(memory_space=pltpu.VMEM)


def shape(*dims):
    return jax.ShapeDtypeStruct(dims, F32)


def swap_sum(x, axis, size, first=0):
    step = 1 << first
    while step < size:
        x = x + lax.ppermute(x, axis, [(i, i ^ step) for i in range(size)])
        step *= 2
    return x


def shards(n_region, n_super, obs_coords, obs_values, obs_precision, site_coords, length_scale,
           global_knots, region_knots, leaf_knots, global_prior, region_prior, leaf_prior):
    r = global_knots.shape[1]
    fields, nobs = obs_values.shape
    knots = jnp.concatenate([global_knots, region_knots[0], leaf_knots[0]], axis=1).T
    width = 512
    chunks = nobs // width
    rows, upper, solved = pl.pallas_call(
        functools.partial(leaf_kernel, chunks),
        out_shape=(shape(r, 2 * r + fields), shape(r, r + fields), shape(r, 2 * r + fields)),
        in_specs=[SMEM] + [VMEM] * 5,
        out_specs=(VMEM,) * 3,
        scratch_shapes=[
            pltpu.VMEM((3 * r + fields, width), jnp.bfloat16),
            pltpu.VMEM((3 * r + fields, width), jnp.bfloat16),
            pltpu.VMEM((3 * r + fields, r), F32),
            pltpu.VMEM((2 * r + fields, r), F32),
            pltpu.VMEM((r + fields, r), F32),
        ],
        name="leaf",
    )(length_scale, knots, obs_coords, obs_values, obs_precision[None, :], leaf_prior[0])
    half = (lax.axis_index("super") & 1).astype(jnp.int32)[None]
    pair = [(i, i ^ 1) for i in range(n_super)]
    own = rows
    step = 1
    other = lax.ppermute(own, "region", [(i, i ^ step) for i in range(n_region)])
    while step * 2 < n_region:
        own = own + other
        step *= 2
        other = lax.ppermute(own, "region", [(i, i ^ step) for i in range(n_region)])
    h = r // 2
    region_solved, keep, send = pl.pallas_call(
        functools.partial(region_kernel, 1.0 / n_region),
        out_shape=(shape(r, r + fields), shape(h, r + fields), shape(h, r + fields)),
        in_specs=[SMEM] + [VMEM] * 4,
        out_specs=(VMEM,) * 3,
        scratch_shapes=[pltpu.VMEM((r, r + fields), F32)],
        name="region",
    )(half, own, other, region_prior[0], upper)
    mine = keep + lax.ppermute(send, "super", pair)
    mine = swap_sum(mine, "region", n_region)
    mine = swap_sum(mine, "super", n_super, first=1)
    other = lax.ppermute(mine, "super", pair)
    table = jnp.concatenate(
        [
            basis_cols(global_knots, site_coords, length_scale[0]),
            basis_cols(region_knots[0], site_coords, length_scale[1]),
            basis_cols(leaf_knots[0], site_coords, length_scale[2]),
        ],
        axis=0,
    )
    return pl.pallas_call(
        global_kernel,
        out_shape=shape(fields, site_coords.shape[1]),
        in_specs=[SMEM] + [VMEM] * 6,
        out_specs=VMEM,
        scratch_shapes=[pltpu.VMEM((r, r + fields), F32)],
        name="predict",
    )(half, mine, other, global_prior, region_solved, solved, table)


def solution(mesh):
    in_specs = (
        P(None, ("region", "super")),
        P(None, ("region", "super")),
        P(("region", "super")),
        P(None, ("region", "super")),
        P(),
        P(),
        P("super", None, None),
        P(("region", "super"), None, None),
        P(),
        P("super", None, None),
        P(("region", "super"), None, None),
    )
    out_specs = P(None, ("region", "super"))
    body = functools.partial(shards, mesh.shape["region"], mesh.shape["super"])
    return jax.shard_map(body, mesh=mesh, in_specs=in_specs, out_specs=out_specs, check_vma=False)
```

time: 378 us -> 104 us (0.28); the launches traced: 374 us -> 104 us
  other arithmetic: 172 us -> 3.58 us
  waiting for transfers between devices: 134 us -> 34.4 us
  Pallas kernels: 0 us -> 46 us
  matrix products: 25 us -> 0 us
  between operations: 21.9 us -> 3.9 us
  local copies, waits for them, and re-layouts: 20.4 us -> 4.7 us
  starting transfers between devices: 0.22 us -> 11.4 us
    another operation x27 -> x0, other arithmetic: 163 us -> none  [the longest x7 34.9 us: shards(): factor = jnp.linalg.cholesky(global_prior + upper[:, :R])]
    psum x2 -> x0, waiting for transfers between devices: 134 us -> none  [the longest x1 89 us: shards(): upper = lax.psum(global_part(summed) - correction, 'super')]
    pallas_call x0 -> x3, Pallas kernels: none -> 46 us  [the longest x1 20.2 us: shards(): pl.pallas_call(functools.partial(leaf_kernel, chunks), out_shape=(shape(r...]
    ppermute x0 -> x7, waiting for transfers between devices: none -> 34.4 us  [the longest x4 21.1 us: swap_sum(): x = x + lax.ppermute(x, axis, [(i, i ^ step) for i in range(size)])]
    dot_general x6 -> x0, matrix products: 15.8 us -> none  [the longest x1 8.01 us: leaf_terms(): lax.dot_general(scaled, scaled, (((0,), (0,)), ((), ())), preferred_eleme...]
    another operation x25 -> x0, local copies, waits for them, and re-layouts: 11.9 us -> none
    ppermute x0 -> x7, starting transfers between devices: none -> 11.4 us  [the longest x4 8.3 us: swap_sum(): x = x + lax.ppermute(x, axis, [(i, i ^ step) for i in range(size)])]
    another operation x24 -> x0, matrix products: 9.2 us -> none  [the longest x6 2.92 us: shards(): global_weights = jax.scipy.linalg.cho_solve((factor, True), upper[:, R:])]
  transfers between devices with their start and end apart: 2 -> 7, of which waited for: 2 -> 5; matrix products, arithmetic and copies ran while one was open for 0% -> 2% of each run, Pallas kernels for 0% -> 0%
where the time goes in v1:
time: 104 us
  Pallas kernels  46 us (44%)
  waiting for transfers between devices  34.4 us (33%)
  starting transfers between devices  11.4 us (11%)
  local copies, waits for them, and re-layouts  4.7 us (5%)
  between operations  3.9 us (4%)
  other arithmetic  3.58 us (3%)
    ppermute x4, waiting for transfers between devices, swap_sum(): x = x + lax.ppermute(x, axis, [(i, i ^ step) for i in range(size)])  21.1 us
    pallas_call x1, Pallas kernels, shards(): pl.pallas_call(functools.partial(leaf_kernel, chunks), out_shape=(shape(r...  20.2 us
    pallas_call x1, Pallas kernels, shards(): pl.pallas_call(global_kernel, out_shape=shape(fields, site_coords.shape[1...  13.6 us
    ppermute x1, waiting for transfers between devices, shards(): lax.ppermute(own, 'region', [(i, i ^ step) for i in range(n_region)])  13.3 us
    pallas_call x1, Pallas kernels, shards(): pl.pallas_call(functools.partial(region_kernel, 1.0 / n_region), out_shap...  12.2 us
    ppermute x4, starting transfers between devices, swap_sum(): x = x + lax.ppermute(x, axis, [(i, i ^ step) for i in range(size)])  8.3 us
    ppermute x1, starting transfers between devices, shards(): lax.ppermute(own, 'region', [(i, i ^ step) for i in range(n_region)])  3.04 us
  transfers between devices with their start and end apart: 7, of which 5 were waited for; matrix products, arithmetic and copies ran while one was open for 2% of the time, Pallas kernels for 0%

profile of v1, /device:TPU:0, one launch (start us, length us, event | category | flops | bytes accessed | tf_op | source)
XLA Modules:
  0.0 104.0 jit_solution(17133728378883165637)
XLA Ops:
  0.0 0.7 pad_maximum_fusion.1
  0.7 0.9 copy.15
  1.7 20.2 %leaf.1 = (f32[256,576]{1,0:T(8,128)}, f32[256,320]{1,0:T(8,128)}, f32[256,576]{1,0:T(8,128)}) custom-call(f32[3]{0:T(128)} %scale_ref.1, f32[768,2]{1,0:T(8,128)} %bitcast.18, f32[2,4096]{1,0:T(2,128)} %coords_ref.1, bf16[64,4096]{1,0:T(8,128)(2,1)} %values_ref.1, f32[1,4096]{1,0:T(1,128)} %bitcast.21, f32[256,256]{1,0:T(8,128)} %bitcast.20), custom_call_target="tpu_custom_call" | custom-call | tf_op jit(solution)/shard_map/leaf/pallas_call | solution.py:168
  21.8 1.3 %copy.16 = f32[256,576]{0,1:T(8,128)S(1)} copy(f32[256,576]{1,0:T(8,128)} %get-tuple-element.11.own_ref) | data formatting | bytes 1179648 | tf_op jit(solution)/shard_map/leaf/pallas_call | solution.py:168
  23.1 3.0 %collective-permute-start = (f32[256,576]{0,1:T(8,128)S(1)}, f32[256,576]{0,1:T(8,128)S(1)}, u32[]{:S(2)}, u32[]{:S(2)}) collective-permute-start(f32[256,576]{0,1:T(8,128)S(1)} %copy.16), channel_id=1, source_target_pairs={{0,16},{16,0},{1,17},{17,1},{2,18},{18,2},{3,19},{19,3},{4,20},{20... | collective-permute-start | bytes 1769480 | tf_op jit(solution)/shard_map/ppermute | solution.py:186
  26.2 13.3 %collective-permute-done = f32[256,576]{0,1:T(8,128)S(1)} collective-permute-done((f32[256,576]{0,1:T(8,128)S(1)}, f32[256,576]{0,1:T(8,128)S(1)}, u32[]{:S(2)}, u32[]{:S(2)}) %collective-permute-start) | collective-permute-done | bytes 589856 | tf_op jit(solution)/shard_map/ppermute | solution.py:186
  39.5 1.1 %copy.17.other_ref = f32[256,576]{1,0:T(8,128)} copy(f32[256,576]{0,1:T(8,128)S(1)} %collective-permute-done) | data formatting | bytes 1179648 | tf_op jit(solution)/shard_map/ppermute | solution.py:186
  40.6 12.2 %region.1 = (f32[256,320]{1,0:T(8,128)}, f32[128,320]{1,0:T(8,128)}, f32[128,320]{1,0:T(8,128)}) custom-call(s32[1]{0:T(128)} %bitcast.half_ref, f32[256,576]{1,0:T(8,128)} %get-tuple-element.11.own_ref, f32[256,576]{1,0:T(8,128)} %copy.17.other_ref, f32[256,256]{1,0:T(8,128)} %bitcast.19, f32[256,320]{1,0:T(8,128)} %get-tuple-element.12.upper_ref), custom_call_target="tpu_custom_call" | custom-call | tf_op jit(solution)/shard_map/region/pallas_call | solution.py:192
  52.9 0.0 collective-permute-start.1
  52.9 0.0 copy-done.2
  52.9 0.7 fusion.4
  57.3 0.0 collective-permute-done.1
  57.4 1.0 add.24
  58.3 1.8 %collective-permute-start.2 = (f32[128,320]{1,0:T(8,128)S(1)}, f32[128,320]{1,0:T(8,128)S(1)}, u32[]{:S(2)}, u32[]{:S(2)}) collective-permute-start(f32[128,320]{1,0:T(8,128)S(1)} %add.24), channel_id=1, source_target_pairs={{0,16},{16,0},{1,17},{17,1},{2,18},{18,2},{3,19},{19,3},{4,20},{20... | collective-permute-start | bytes 491528 | tf_op jit(solution)/shard_map/ppermute | solution.py:156
  60.1 0.0 copy-done.6
  60.1 5.6 %collective-permute-done.2 = f32[128,320]{1,0:T(8,128)S(1)} collective-permute-done((f32[128,320]{1,0:T(8,128)S(1)}, f32[128,320]{1,0:T(8,128)S(1)}, u32[]{:S(2)}, u32[]{:S(2)}) %collective-permute-start.2) | collective-permute-done | bytes 163872 | tf_op jit(solution)/shard_map/ppermute | solution.py:156
  65.7 1.8 %collective-permute-start.3 = (f32[128,320]{1,0:T(8,128)S(1)}, f32[128,320]{1,0:T(8,128)S(1)}, u32[]{:S(2)}, u32[]{:S(2)}) collective-permute-start(f32[128,320]{1,0:T(8,128)S(1)} %add.25), channel_id=1, source_target_pairs={{0,2},{1,3},{2,0},{3,1},{4,6},{5,7},{6,4},{7,5},{8,10},{9,11},{10,... | collective-permute-start | bytes 491528 | tf_op jit(solution)/shard_map/ppermute | solution.py:156
  67.5 0.0 copy-done.3
  67.5 4.7 %collective-permute-done.3 = f32[128,320]{1,0:T(8,128)S(1)} collective-permute-done((f32[128,320]{1,0:T(8,128)S(1)}, f32[128,320]{1,0:T(8,128)S(1)}, u32[]{:S(2)}, u32[]{:S(2)}) %collective-permute-start.3) | collective-permute-done | bytes 163872 | tf_op jit(solution)/shard_map/ppermute | solution.py:156
  72.3 1.9 %collective-permute-start.4 = (f32[128,320]{1,0:T(8,128)S(1)}, f32[128,320]{1,0:T(8,128)S(1)}, u32[]{:S(2)}, u32[]{:S(2)}) collective-permute-start(f32[128,320]{1,0:T(8,128)S(1)} %add.26), channel_id=1, source_target_pairs={{0,4},{1,5},{2,6},{3,7},{4,0},{5,1},{6,2},{7,3},{8,12},{9,13},{10,... | collective-permute-start | bytes 491528 | tf_op jit(solution)/shard_map/ppermute | solution.py:156
  74.1 0.0 copy-done.4
  74.1 3.9 %collective-permute-done.4 = f32[128,320]{1,0:T(8,128)S(1)} collective-permute-done((f32[128,320]{1,0:T(8,128)S(1)}, f32[128,320]{1,0:T(8,128)S(1)}, u32[]{:S(2)}, u32[]{:S(2)}) %collective-permute-start.4) | collective-permute-done | bytes 163872 | tf_op jit(solution)/shard_map/ppermute | solution.py:156
  78.0 2.9 %collective-permute-start.5 = (f32[128,320]{1,0:T(8,128)S(1)}, f32[128,320]{1,0:T(8,128)S(1)}, u32[]{:S(2)}, u32[]{:S(2)}) collective-permute-start(f32[128,320]{1,0:T(8,128)S(1)} %add.27), channel_id=1, source_target_pairs={{0,8},{1,9},{2,10},{3,11},{4,12},{5,13},{6,14},{7,15},{8,0},{9,1},... | collective-permute-start | bytes 491528 | tf_op jit(solution)/shard_map/ppermute | solution.py:156
  80.9 0.0 copy-done.5
  80.9 6.9 %collective-permute-done.5 = f32[128,320]{1,0:T(8,128)S(1)} collective-permute-done((f32[128,320]{1,0:T(8,128)S(1)}, f32[128,320]{1,0:T(8,128)S(1)}, u32[]{:S(2)}, u32[]{:S(2)}) %collective-permute-start.5) | collective-permute-done | bytes 163872 | tf_op jit(solution)/shard_map/ppermute | solution.py:156
  87.8 0.1 collective-permute-start.6
  87.9 0.5 divide_exponential_fusion.2
  88.5 1.3 %pad_maximum_fusion.table_ref = f32[768,512]{1,0:T(8,128)} fusion(f32[256,512]{1,0:T(8,128)S(1)} %get-tuple-element.19, f32[256,512]{1,0:T(8,128)S(1)} %get-tuple-element.18, f32[256,512]{1,0:T(8,128)S(1)} %get-tuple-element.17), kind=kLoop, calls=%fused_computation | loop fusion | flops 786432 | bytes 3145728 | tf_op jit(solution)/shard_map/concatenate | solution.py:204
  89.7 0.0 copy-done
  89.7 0.0 collective-permute-done.6.other_ref
  89.7 0.7 copy-done.1
  90.4 13.6 %predict.1 = f32[64,512]{1,0:T(8,128)} custom-call(s32[1]{0:T(128)} %bitcast.half_ref, f32[128,320]{1,0:T(8,128)} %copy-done, f32[128,320]{1,0:T(8,128)} %copy-done.1, f32[256,256]{1,0:T(8,128)} %prior_ref.1, f32[256,320]{1,0:T(8,128)} %get-tuple-element.15.region_ref, f32[256,576]{1,0:T(8,128)} %get-tuple-element.16.leaf_ref, ...), custom_call_target="tpu_custom_call" | custom-call | tf_op jit(solution)/shard_map/predict/pallas_call | solution.py:212
  (15 shorter events, 0.1 us)
Async XLA Ops:
  23.1 16.4 %collective-permute-start = (f32[256,576]{0,1:T(8,128)S(1)}, f32[256,576]{0,1:T(8,128)S(1)}, u32[]{:S(2)}, u32[]{:S(2)}) collective-permute-start(f32[256,576]{0,1:T(8,128)S(1)} %copy.16), channel_id=1, source_target_pairs={{0,16},{16,0},{1,17},{17,1},{2,18},{18,2},{3,19},{19,3},{4,20},{20... | collective-permute-start | bytes 1769480 | tf_op jit(solution)/shard_map/ppermute | solution.py:186
  26.2 26.7 %copy-start.2 = (f32[3]{0:T(128)S(1)}, f32[3]{0:T(128)}, u32[]{:S(2)}) copy-start(f32[3]{0:T(128)} %scale_ref.1) | copy-start | bytes 40
  40.6 19.5 %copy-start.6 = (f32[2,512]{1,0:T(2,128)S(1)}, f32[2,512]{1,0:T(2,128)}, u32[]{:S(2)}) copy-start(f32[2,512]{1,0:T(2,128)} %param.14) | copy-start | bytes 12292
  40.6 26.9 %copy-start.3 = (f32[2,256]{1,0:T(2,128)S(1)}, f32[2,256]{1,0:T(2,128)}, u32[]{:S(2)}) copy-start(f32[2,256]{1,0:T(2,128)} %param.16) | copy-start | bytes 6148
  40.6 33.5 %copy-start.4 = (f32[1,2,256]{2,1,0:T(2,128)S(1)}, f32[1,2,256]{2,1,0:T(2,128)}, u32[]{:S(2)}) copy-start(f32[1,2,256]{2,1,0:T(2,128)} %param.17) | copy-start | bytes 6148
  52.9 28.0 %copy-start.5 = (f32[1,2,256]{2,1,0:T(2,128)S(1)}, f32[1,2,256]{2,1,0:T(2,128)}, u32[]{:S(2)}) copy-start(f32[1,2,256]{2,1,0:T(2,128)} %param.18) | copy-start | bytes 6148
  52.9 4.5 %collective-permute-start.1 = (f32[128,320]{1,0:T(8,128)}, f32[128,320]{1,0:T(8,128)S(1)}, u32[]{:S(2)}, u32[]{:S(2)}) collective-permute-start(f32[128,320]{1,0:T(8,128)} %get-tuple-element.14), channel_id=1, source_target_pairs={{0,1},{1,0},{2,3},{3,2},{4,5},{5,4},{6,7},{7,6},{8,9},{9,8},{10,11... | collective-permute-start | bytes 491528 | tf_op jit(solution)/shard_map/ppermute | solution.py:200
  58.3 7.4 %collective-permute-start.2 = (f32[128,320]{1,0:T(8,128)S(1)}, f32[128,320]{1,0:T(8,128)S(1)}, u32[]{:S(2)}, u32[]{:S(2)}) collective-permute-start(f32[128,320]{1,0:T(8,128)S(1)} %add.24), channel_id=1, source_target_pairs={{0,16},{16,0},{1,17},{17,1},{2,18},{18,2},{3,19},{19,3},{4,20},{20... | collective-permute-start | bytes 491528 | tf_op jit(solution)/shard_map/ppermute | solution.py:156
  65.7 6.5 %collective-permute-start.3 = (f32[128,320]{1,0:T(8,128)S(1)}, f32[128,320]{1,0:T(8,128)S(1)}, u32[]{:S(2)}, u32[]{:S(2)}) collective-permute-start(f32[128,320]{1,0:T(8,128)S(1)} %add.25), channel_id=1, source_target_pairs={{0,2},{1,3},{2,0},{3,1},{4,6},{5,7},{6,4},{7,5},{8,10},{9,11},{10,... | collective-permute-start | bytes 491528 | tf_op jit(solution)/shard_map/ppermute | solution.py:156
  72.3 5.7 %collective-permute-start.4 = (f32[128,320]{1,0:T(8,128)S(1)}, f32[128,320]{1,0:T(8,128)S(1)}, u32[]{:S(2)}, u32[]{:S(2)}) collective-permute-start(f32[128,320]{1,0:T(8,128)S(1)} %add.26), channel_id=1, source_target_pairs={{0,4},{1,5},{2,6},{3,7},{4,0},{5,1},{6,2},{7,3},{8,12},{9,13},{10,... | collective-permute-start | bytes 491528 | tf_op jit(solution)/shard_map/ppermute | solution.py:156
  78.0 9.8 %collective-permute-start.5 = (f32[128,320]{1,0:T(8,128)S(1)}, f32[128,320]{1,0:T(8,128)S(1)}, u32[]{:S(2)}, u32[]{:S(2)}) collective-permute-start(f32[128,320]{1,0:T(8,128)S(1)} %add.27), channel_id=1, source_target_pairs={{0,8},{1,9},{2,10},{3,11},{4,12},{5,13},{6,14},{7,15},{8,0},{9,1},... | collective-permute-start | bytes 491528 | tf_op jit(solution)/shard_map/ppermute | solution.py:156
  87.8 1.9 %copy-start = (f32[128,320]{1,0:T(8,128)}, f32[128,320]{1,0:T(8,128)S(1)}, u32[]{:S(2)}) copy-start(f32[128,320]{1,0:T(8,128)S(1)} %add.28.mine_ref) | copy-start | bytes 491524
  87.8 1.9 %collective-permute-start.6 = (f32[128,320]{1,0:T(8,128)S(1)}, f32[128,320]{1,0:T(8,128)S(1)}, u32[]{:S(2)}, u32[]{:S(2)}) collective-permute-start(f32[128,320]{1,0:T(8,128)S(1)} %add.28.mine_ref), channel_id=1, source_target_pairs={{0,1},{1,0},{2,3},{3,2},{4,5},{5,4},{6,7},{7,6},{8,9},{9,8},{10,11... | collective-permute-start | bytes 491528 | tf_op jit(solution)/shard_map/ppermute | solution.py:203
  89.7 0.7 copy-start.1

commit v2 on v1

v2 whole, which is shorter than its diff:
```python
import functools

import jax
import jax.numpy as jnp
from jax import lax
from jax.experimental import pallas as pl
from jax.experimental.pallas import tpu as pltpu
from jax.sharding import PartitionSpec as P


HIGH = lax.Precision.HIGHEST
F32 = jnp.float32


def mm(a, b, ca=1, cb=0):
    return lax.dot_general(a, b, (((ca,), (cb,)), ((), ())), precision=HIGH, preferred_element_type=F32)


def spd_inverse(a):
    n = a.shape[0]
    groups = n // 8
    rows = [a[8 * i : 8 * i + 8, :] for i in range(groups)]
    lane = lax.broadcasted_iota(jnp.int32, (8, n), 1)
    sub = lax.broadcasted_iota(jnp.int32, (8, n), 0)
    for g in range(groups):

        def col(x, k, g=g):
            return jnp.broadcast_to(x[:, 8 * g + k : 8 * g + k + 1], (8, n))

        p = rows[g]
        c = [col(p, k) for k in range(8)]
        inside = (lane >= 8 * g) & (lane < 8 * g + 8)
        p = jnp.where(inside, jnp.where(lane - 8 * g == sub, 1.0, 0.0), p)
        for k in range(8):
            here = sub == k
            r = 1.0 / jnp.broadcast_to(c[k][k : k + 1, :], (8, n))
            for m in range(k + 1, 8):
                s = jnp.broadcast_to(c[m][k : k + 1, :], (8, n)) * r
                c[m] = jnp.where(here, s, c[m] - c[k] * s)
            s = jnp.broadcast_to(p[k : k + 1, :], (8, n)) * r
            p = jnp.where(here, s, p - c[k] * s)
        pr = [jnp.broadcast_to(p[k : k + 1, :], (8, n)) for k in range(8)]
        for i in range(groups):
            if i == g:
                continue
            old = rows[i]
            t = [col(old, k) * pr[k] for k in range(8)]
            while len(t) > 1:
                t = [t[q] + t[q + 1] for q in range(0, len(t), 2)]
            rows[i] = jnp.where(inside, 0.0, old) - t[0]
        rows[g] = p
    return jnp.concatenate(rows, axis=0)


def spd_factor(a):
    h = a.shape[0] // 2
    a12 = a[:h, h:]
    i1 = spd_inverse(a[:h, :h])
    t = mm(i1, a12)
    i2 = spd_inverse(a[h:, h:] - mm(a12, t, 0, 0))
    return i1, t, i2


def spd_apply(factor, b):
    i1, t, i2 = factor
    h = t.shape[0]
    x2 = mm(i2, b[h:] - mm(t, b[:h], 0, 0))
    x1 = mm(i1, b[:h]) - mm(t, x2)
    return jnp.concatenate([x1, x2], axis=0)


def pack_halves(f):
    h = f.shape[0] // 2
    q = h // 2
    first = jnp.concatenate([f[:h, :h], f[:h, h : h + q], f[:h, 2 * h :]], axis=1)
    second = jnp.concatenate([f[h:, h : 2 * h], f[:h, h + q : 2 * h], f[h:, 2 * h :]], axis=1)
    return first, second


def knot_columns(refs):
    rows = [refs[0][...], refs[1][0], refs[2][0]]
    rows.append(jnp.zeros_like(rows[0]))
    return jnp.transpose(jnp.concatenate(rows, axis=0))


def basis(knots, level, px, py, scale):
    dx = knots[:, 2 * level : 2 * level + 1] - px
    dy = knots[:, 2 * level + 1 : 2 * level + 2] - py
    return jnp.exp((dx * dx + dy * dy) * (-0.5 / (scale * scale)))


def leaf_kernel(chunks, scale_ref, kg_ref, kr_ref, kl_ref, coords_ref, values_ref, prec_ref, prior_ref,
                pair_ref, factor_ref, acc_g, acc_r, acc_v, za, zb, knots_ref):
    r = prior_ref.shape[1]
    h = r // 2
    width = za.shape[1]
    knots_ref[...] = knot_columns((kg_ref, kr_ref, kl_ref))

    def fill(z, chunk):
        cols = pl.ds(pl.multiple_of(chunk * width, width), width)
        px = coords_ref[0:1, cols]
        py = coords_ref[1:2, cols]
        weight = jnp.sqrt(prec_ref[0:1, cols])
        knots = knots_ref[...]
        for level in range(3):
            table = basis(knots, level, px, py, scale_ref[level])
            z[level * r : (level + 1) * r, :] = (table * weight).astype(jnp.bfloat16)
        z[3 * r :, :] = (values_ref[:, cols].astype(F32) * weight).astype(jnp.bfloat16)

    def gram(z):
        for level, acc in enumerate((acc_g, acc_r, acc_v)):
            acc[...] += lax.dot_general(
                z[level * r :, :], z[level * r : (level + 1) * r, :], (((1,), (1,)), ((), ())),
                preferred_element_type=F32,
            )

    acc_g[...] = jnp.zeros_like(acc_g)
    acc_r[...] = jnp.zeros_like(acc_r)
    acc_v[...] = jnp.zeros_like(acc_v)
    fill(za, 0)

    def step(i, carry):
        fill(zb, 2 * i + 1)
        gram(za)
        fill(za, jnp.minimum(2 * i + 2, chunks - 1))
        gram(zb)
        return carry

    lax.fori_loop(0, chunks // 2, step, 0)
    cross = acc_r[r : 2 * r, :]
    factor = spd_factor(prior_ref[0] + acc_v[:r, :])
    for i in range(3):
        factor_ref[i] = factor[i]
    s = acc_r[:r, :] - mm(cross, spd_apply(factor, cross), 0, 0)
    pair_ref[...] = jnp.concatenate([s[:h, :h], s[:h, h:], s[h:, h:]], axis=1)


def leaf_rest_kernel(half_ref, scale_ref, kg_ref, kr_ref, kl_ref, sites_ref, factor_ref, acc_g, acc_r, acc_v,
                     solved_ref, cross_ref, keep_ref, send_ref, table_ref, pieces):
    r = acc_g.shape[1]
    h = r // 2
    y_cols = jnp.transpose(jnp.concatenate([acc_g[3 * r :, :], acc_r[2 * r :, :], acc_v[r:, :]], axis=1))
    cross_g = acc_g[2 * r : 3 * r, :]
    cross_r = acc_r[r : 2 * r, :]
    factor = (factor_ref[0], factor_ref[1], factor_ref[2])
    x = spd_apply(factor, jnp.concatenate([cross_g, cross_r, y_cols[2 * r :]], axis=1))
    solved_ref[...] = x
    x = jnp.concatenate([x[:, :r], x[:, 2 * r :]], axis=1)
    rows = jnp.concatenate([acc_g[r : 2 * r, :], y_cols[r : 2 * r]], axis=1) - mm(cross_r, x, 0, 0)
    cross_ref[...] = jnp.concatenate([rows[:h, :r], rows[h:, :r], rows[:h, r:], rows[h:, r:]], axis=1)
    upper = jnp.concatenate([acc_g[:r, :], y_cols[:r]], axis=1) - mm(cross_g, x, 0, 0)
    pieces[0], pieces[1] = pack_halves(upper)
    keep_ref[...] = pieces[half_ref[0]]
    send_ref[...] = pieces[1 - half_ref[0]]
    knots = knot_columns((kg_ref, kr_ref, kl_ref))
    for level in range(3):
        table_ref[level * r : (level + 1) * r, :] = basis(
            knots, level, sites_ref[0:1, :], sites_ref[1:2, :], scale_ref[level]
        )


def region_factor_kernel(own_ref, other_ref, prior_ref, after_ref, factor_ref):
    h = own_ref.shape[0]
    s = own_ref[...] + other_ref[...]
    lower = jnp.concatenate([s[:, h : 2 * h], s[:, 2 * h :]], axis=0)
    upper = jnp.concatenate([s[:, :h], jnp.zeros_like(s[:, :h])], axis=0)
    factor = spd_factor(prior_ref[0] + jnp.concatenate([upper, lower], axis=1))
    for i in range(3):
        factor_ref[i] = factor[i]


def region_kernel(half_ref, factor_ref, own_ref, other_ref, upper_ref, solved_ref, keep_ref, send_ref, pieces):
    h = own_ref.shape[0]
    r = 2 * h
    rows = own_ref[...] + other_ref[...]
    fields = (rows.shape[1] - 2 * r) // 2
    cross = jnp.concatenate([rows[:, :r], rows[:, r : 2 * r]], axis=0)
    y = jnp.concatenate([rows[:, 2 * r : 2 * r + fields], rows[:, 2 * r + fields :]], axis=0)
    x = spd_apply((factor_ref[0], factor_ref[1], factor_ref[2]), jnp.concatenate([cross, y], axis=1))
    solved_ref[...] = x
    pieces[0], pieces[1] = pack_halves(-mm(cross, x, 0, 0))
    keep_ref[...] = upper_ref[...] + pieces[half_ref[0]]
    send_ref[...] = pieces[1 - half_ref[0]]


def global_kernel(half_ref, mine_ref, other_ref, prior_ref, region_ref, leaf_ref, table_ref, out_ref, pieces):
    r = prior_ref.shape[0]
    h = r // 2
    q = h // 2
    pieces[half_ref[0]] = mine_ref[...]
    pieces[1 - half_ref[0]] = other_ref[...]
    a = pieces[0]
    b = pieces[1]
    top = jnp.concatenate([a[:, : h + q], b[:, h : h + q]], axis=1)
    low = jnp.concatenate([jnp.zeros_like(b[:, :h]), b[:, :h]], axis=1)
    y = jnp.concatenate([a[:, h + q :], b[:, h + q :]], axis=0)
    w_g = spd_apply(spd_factor(prior_ref[...] + jnp.concatenate([top, low], axis=0)), y)
    w_r = region_ref[:, r:] - mm(region_ref[:, :r], w_g)
    w_l = leaf_ref[:, 2 * r :] - mm(leaf_ref[:, : 2 * r], jnp.concatenate([w_g, w_r], axis=0))
    out_ref[...] = mm(jnp.concatenate([w_g, w_r, w_l], axis=0), table_ref[...], 0, 0)


SMEM = pl.BlockSpec(memory_space=pltpu.SMEM)
VMEM = pl.BlockSpec(memory_space=pltpu.VMEM)
ANY = pl.BlockSpec(memory_space=pl.ANY)


def in_vmem(x):
    return pltpu.with_memory_space_constraint(x, pltpu.VMEM)


def shape(*dims):
    return jax.ShapeDtypeStruct(dims, F32)


def cost(flops, transcendentals):
    return pl.CostEstimate(flops=6 * flops, transcendentals=transcendentals, bytes_accessed=1 << 21)


def swap(x, axis, size, mask):
    return lax.ppermute(x, axis, [(i, i ^ mask) for i in range(size)])


def masks(size, first):
    bits = [b for b in range(first, size.bit_length() - 1)]
    return [(3 << (b - 1)) if b >= 3 else (1 << b) for b in bits]


def swap_halfway(x, axis, size):
    steps = masks(size, 0)
    for mask in steps[:-1]:
        x = x + swap(x, axis, size, mask)
    return x, swap(x, axis, size, steps[-1])


def shards(n_region, n_super, obs_coords, obs_values, obs_precision, site_coords, length_scale,
           global_knots, region_knots, leaf_knots, global_prior, region_prior, leaf_prior):
    r = global_knots.shape[1]
    h = r // 2
    fields, nobs = obs_values.shape
    nsite = site_coords.shape[1]
    width = 512
    knots = (global_knots, region_knots, leaf_knots)
    half = (lax.axis_index("super") & 1).astype(jnp.int32)[None]
    tall = [shape((3 - level) * r + fields, r) for level in range(3)]
    z = pltpu.VMEM((3 * r + fields, width), jnp.bfloat16)
    own, factor, acc_g, acc_r, acc_v = pl.pallas_call(
        functools.partial(leaf_kernel, nobs // width),
        out_shape=(shape(h, 3 * h), shape(3, h, h), *tall),
        in_specs=[SMEM] + [VMEM] * 7,
        out_specs=(VMEM,) * 5,
        scratch_shapes=[z, z, pltpu.VMEM((r, 8), F32)],
        name="leaf",
        cost_estimate=cost(2 * nobs * (3 * r + fields) ** 2, 3 * r * nobs),
    )(length_scale, *knots, obs_coords, obs_values, obs_precision[None, :], leaf_prior)
    own, other = swap_halfway(own, "region", n_region)
    pieces = pltpu.VMEM((2, h, r), F32)
    solved, cross, keep, send, table = pl.pallas_call(
        leaf_rest_kernel,
        out_shape=(shape(r, 2 * r + fields), shape(h, 2 * r + 2 * fields), shape(h, r), shape(h, r), shape(3 * r, nsite)),
        in_specs=[SMEM] * 2 + [VMEM] * 8,
        out_specs=(VMEM,) * 5,
        scratch_shapes=[pieces],
        name="leaf_rest",
        cost_estimate=cost(r * r * (8 * r + 6 * fields), 3 * r * nsite),
    )(half, length_scale, *knots, site_coords, factor, acc_g, acc_r, acc_v)
    region_factor = pl.pallas_call(
        region_factor_kernel,
        out_shape=shape(3, h, h),
        in_specs=[VMEM] * 3 + [ANY],
        out_specs=VMEM,
        name="region_factor",
        cost_estimate=cost(8 * r * r * r, r),
    )(own, in_vmem(other), region_prior, table)
    own, other = swap_halfway(cross, "region", n_region)
    upper = keep + swap(send, "super", n_super, 1)
    for mask in masks(n_region, 0):
        upper = upper + swap(upper, "region", n_region, mask)
    region_solved, keep, send = pl.pallas_call(
        region_kernel,
        out_shape=(shape(r, r + fields), shape(h, r), shape(h, r)),
        in_specs=[SMEM] + [VMEM] * 4,
        out_specs=(VMEM,) * 3,
        scratch_shapes=[pieces],
        name="region",
        cost_estimate=cost(4 * r * r * (r + fields), r),
    )(half, region_factor, own, in_vmem(other), in_vmem(upper))
    mine = keep + swap(send, "super", n_super, 1)
    for mask in masks(n_super, 1):
        mine = mine + swap(mine, "super", n_super, mask)
    other = swap(mine, "super", n_super, 1)
    return pl.pallas_call(
        global_kernel,
        out_shape=shape(fields, nsite),
        in_specs=[SMEM] + [VMEM] * 6,
        out_specs=VMEM,
        scratch_shapes=[pieces],
        name="predict",
        cost_estimate=cost(8 * r * r * r, r),
    )(half, in_vmem(mine), in_vmem(other), global_prior, region_solved, solved, table)


def solution(mesh):
    in_specs = (
        P(None, ("region", "super")),
        P(None, ("region", "super")),
        P(("region", "super")),
        P(None, ("region", "super")),
        P(),
        P(),
        P("super", None, None),
        P(("region", "super"), None, None),
        P(),
        P("super", None, None),
        P(("region", "super"), None, None),
    )
    out_specs = P(None, ("region", "super"))
    body = functools.partial(shards, mesh.shape["region"], mesh.shape["super"])

    return jax.shard_map(body, mesh=mesh, in_specs=in_specs, out_specs=out_specs, check_vma=False)
```

time: 104 us -> 89.9 us (0.86)
  waiting for transfers between devices: 34.4 us -> 22.9 us
  Pallas kernels: 46 us -> 51.8 us
  local copies, waits for them, and re-layouts: 4.7 us -> 0.01 us
  between operations: 3.9 us -> 0.05 us
  other arithmetic: 3.58 us -> 1.91 us
  starting transfers between devices: 11.4 us -> 13 us
    ppermute x7 -> x9, waiting for transfers between devices: 34.4 us -> 22.9 us  [swap(): return lax.ppermute(x, axis, [(i, i ^ mask) for i in range(size)])]
    pallas_call x3 -> x5, Pallas kernels: 46 us -> 51.8 us  [the longest x1 18.9 us: shards(): pl.pallas_call(functools.partial(leaf_kernel, nobs // width), out_shape=(...]
    concatenate x2 -> x0, other arithmetic: 2 us -> none  [the longest x1 1.28 us: shards(): jnp.concatenate([basis_cols(global_knots, site_coords, length_scale[0]),...]
    ppermute x7 -> x9, starting transfers between devices: 11.4 us -> 13 us  [swap(): return lax.ppermute(x, axis, [(i, i ^ mask) for i in range(size)])]
    pallas_call x1 -> x0, local copies, waits for them, and re-layouts: 1.3 us -> none  [shards(): pl.pallas_call(functools.partial(leaf_kernel, chunks), out_shape=(shape(r...]
    ppermute x1 -> x0, local copies, waits for them, and re-layouts: 1.08 us -> none  [shards(): lax.ppermute(own, 'region', [(i, i ^ step) for i in range(n_region)])]
  transfers between devices with their start and end apart: 7 -> 9, of which waited for: 5 -> 7; matrix products, arithmetic and copies ran while one was open for 2% -> 1% of each run, Pallas kernels for 0% -> 12%
where the time goes in v2:
time: 89.9 us; the launch traced here: 89.6 us
  Pallas kernels  51.8 us (58%)
  waiting for transfers between devices  22.9 us (25%)
  starting transfers between devices  13 us (14%)
  other arithmetic  1.91 us (2%)
    ppermute x9, waiting for transfers between devices, swap(): return lax.ppermute(x, axis, [(i, i ^ mask) for i in range(size)])  22.9 us
    pallas_call x1, Pallas kernels, shards(): pl.pallas_call(functools.partial(leaf_kernel, nobs // width), out_shape=(...  18.9 us
    pallas_call x1, Pallas kernels, shards(): pl.pallas_call(global_kernel, out_shape=shape(fields, nsite), in_specs=[S...  13.5 us
    ppermute x9, starting transfers between devices, swap(): return lax.ppermute(x, axis, [(i, i ^ mask) for i in range(size)])  13 us
    pallas_call x1, Pallas kernels, shards(): pl.pallas_call(region_factor_kernel, out_shape=shape(3, h, h), in_specs=[...  10.6 us
    pallas_call x1, Pallas kernels, shards(): pl.pallas_call(leaf_rest_kernel, out_shape=(shape(r, 2 * r + fields), sha...  5.31 us
    pallas_call x1, Pallas kernels, shards(): pl.pallas_call(region_kernel, out_shape=(shape(r, r + fields), shape(h, r...  3.51 us
  transfers between devices with their start and end apart: 9, of which 7 were waited for; matrix products, arithmetic and copies ran while one was open for 1% of the time, Pallas kernels for 12%

profile of v2, /device:TPU:0, one launch (start us, length us, event | category | flops | bytes accessed | tf_op | source)
XLA Modules:
  0.0 89.6 jit_solution(10022752325339804919)
XLA Ops:
  0.0 18.9 %leaf.1 = (f32[128,384]{1,0:T(8,128)}, f32[3,128,128]{2,1,0:T(8,128)}, f32[832,256]{1,0:T(8,128)}, f32[576,256]{1,0:T(8,128)}, f32[320,256]{1,0:T(8,128)}) custom-call(f32[3]{0:T(128)} %scale_ref.3, f32[2,256]{1,0:T(2,128)} %kg_ref.3, f32[1,2,256]{2,1,0:T(2,128)} %kr_ref.3, f32[1,2,256]{2,1,0:T(2,128)} %kl_ref.3, f32[2,4096]{1,0:T(2,128)} %coords_ref.1, ...), custom_call_target="tpu_custom_call" | custom-call | flops 34024194048 | bytes 2097152 | tf_op jit(solution)/shard_map/leaf/pallas_call | solution.py:247
  18.9 0.0 copy-start
  18.9 5.3 %leaf_rest.1 = (f32[256,576]{1,0:T(8,128)}, f32[128,640]{1,0:T(8,128)}, f32[128,256]{1,0:T(8,128)}, f32[128,256]{1,0:T(8,128)}, f32[768,512]{1,0:T(8,128)}) custom-call(s32[1]{0:T(128)} %bitcast.half_ref, f32[3]{0:T(128)} %scale_ref.3, f32[2,256]{1,0:T(2,128)} %kg_ref.3, f32[1,2,256]{2,1,0:T(2,128)} %kr_ref.3, f32[1,2,256]{2,1,0:T(2,128)} %kl_ref.3, ...), custom_call_target="tpu_custom_call" | custom-call | flops 956301312 | bytes 2097152 | tf_op jit(solution)/shard_map/leaf_rest/pallas_call | solution.py:258
  24.2 3.0 %collective-permute-start.1 = (f32[128,640]{1,0:T(8,128)}, f32[128,640]{1,0:T(8,128)S(1)}, u32[]{:S(2)}, u32[]{:S(2)}) collective-permute-start(f32[128,640]{1,0:T(8,128)} %get-tuple-element.24.own_ref), channel_id=1, source_target_pairs={{0,16},{16,0},{1,17},{17,1},{2,18},{18,2},{3,19},{19,3},{4,20},{20... | collective-permute-start | bytes 983048 | tf_op jit(solution)/shard_map/ppermute | solution.py:221
  27.1 0.0 copy-done
  27.2 0.1 collective-permute-start
  27.2 0.0 collective-permute-start.2
  27.2 1.6 %collective-permute-done.2 = f32[128,256]{1,0:T(8,128)S(1)} collective-permute-done((f32[128,256]{1,0:T(8,128)}, f32[128,256]{1,0:T(8,128)S(1)}, u32[]{:S(2)}, u32[]{:S(2)}) %collective-permute-start.2) | collective-permute-done | bytes 131104 | tf_op jit(solution)/shard_map/ppermute | solution.py:221
  28.8 0.9 %add.18 = f32[128,256]{1,0:T(8,128)S(1)} add(f32[128,256]{1,0:T(8,128)} %get-tuple-element.25, f32[128,256]{1,0:T(8,128)S(1)} %collective-permute-done.2) | non-fusion elementwise | flops 32768 | bytes 393216 | tf_op jit(solution)/shard_map/add | solution.py:276
  29.7 2.0 %collective-permute-start.3 = (f32[128,256]{1,0:T(8,128)S(1)}, f32[128,256]{1,0:T(8,128)S(1)}, u32[]{:S(2)}, u32[]{:S(2)}) collective-permute-start(f32[128,256]{1,0:T(8,128)S(1)} %add.18), channel_id=1, source_target_pairs={{0,16},{16,0},{1,17},{17,1},{2,18},{18,2},{3,19},{19,3},{4,20},{20... | collective-permute-start | bytes 393224 | tf_op jit(solution)/shard_map/ppermute | solution.py:221
  31.7 8.4 %collective-permute-done.other_ref = f32[128,384]{1,0:T(8,128)S(1)} collective-permute-done((f32[128,384]{1,0:T(8,128)S(1)}, f32[128,384]{1,0:T(8,128)S(1)}, u32[]{:S(2)}, u32[]{:S(2)}) %collective-permute-start) | collective-permute-done | bytes 196640 | tf_op jit(solution)/shard_map/ppermute | solution.py:221
  40.1 10.6 %region_factor.1.factor_ref = f32[3,128,128]{2,1,0:T(8,128)} custom-call(f32[128,384]{1,0:T(8,128)} %get-tuple-element.18.own_ref, f32[128,384]{1,0:T(8,128)S(1)} %collective-permute-done.other_ref, f32[1,256,256]{2,1,0:T(8,128)} %prior_ref.4, f32[768,512]{1,0:T(8,128)} %get-tuple-element.23.after_ref.table_ref), custom_call_target="tpu_custom_call" | custom-call | flops 805306368 | bytes 2097152 | tf_op jit(solution)/shard_map/region_factor/pallas_call | solution.py:267
  50.8 0.0 collective-permute-done.3
  50.8 0.0 collective-permute-done.1.other_ref
  50.8 3.5 %region.1 = (f32[256,320]{1,0:T(8,128)}, f32[128,256]{1,0:T(8,128)}, f32[128,256]{1,0:T(8,128)}) custom-call(s32[1]{0:T(128)} %bitcast.half_ref, f32[3,128,128]{2,1,0:T(8,128)} %region_factor.1.factor_ref, f32[128,640]{1,0:T(8,128)} %get-tuple-element.24.own_ref, f32[128,640]{1,0:T(8,128)S(1)} %collective-permute-done.1.other_ref, f32[128,256]{1,0:T(8,128)S(1)} %add.19.upper_ref), custom_call_target="tpu_custom_call" | custom-call | flops 503316480 | bytes 2097152 | tf_op jit(solution)/shard_map/region/pallas_call | solution.py:279
  54.3 0.0 collective-permute-start.4
  54.3 1.6 %collective-permute-done.4 = f32[128,256]{1,0:T(8,128)S(1)} collective-permute-done((f32[128,256]{1,0:T(8,128)}, f32[128,256]{1,0:T(8,128)S(1)}, u32[]{:S(2)}, u32[]{:S(2)}) %collective-permute-start.4) | collective-permute-done | bytes 131104 | tf_op jit(solution)/shard_map/ppermute | solution.py:221
  55.9 0.9 %add.20 = f32[128,256]{1,0:T(8,128)S(1)} add(f32[128,256]{1,0:T(8,128)} %get-tuple-element.27, f32[128,256]{1,0:T(8,128)S(1)} %collective-permute-done.4) | non-fusion elementwise | flops 32768 | bytes 393216 | tf_op jit(solution)/shard_map/add | solution.py:288
  56.8 2.1 %collective-permute-start.5 = (f32[128,256]{1,0:T(8,128)S(1)}, f32[128,256]{1,0:T(8,128)S(1)}, u32[]{:S(2)}, u32[]{:S(2)}) collective-permute-start(f32[128,256]{1,0:T(8,128)S(1)} %add.20), channel_id=1, source_target_pairs={{0,2},{1,3},{2,0},{3,1},{4,6},{5,7},{6,4},{7,5},{8,10},{9,11},{10,... | collective-permute-start | bytes 393224 | tf_op jit(solution)/shard_map/ppermute | solution.py:221
  58.8 3.8 %collective-permute-done.5 = f32[128,256]{1,0:T(8,128)S(1)} collective-permute-done((f32[128,256]{1,0:T(8,128)S(1)}, f32[128,256]{1,0:T(8,128)S(1)}, u32[]{:S(2)}, u32[]{:S(2)}) %collective-permute-start.5) | collective-permute-done | bytes 131104 | tf_op jit(solution)/shard_map/ppermute | solution.py:221
  62.7 1.9 %collective-permute-start.6 = (f32[128,256]{1,0:T(8,128)S(1)}, f32[128,256]{1,0:T(8,128)S(1)}, u32[]{:S(2)}, u32[]{:S(2)}) collective-permute-start(f32[128,256]{1,0:T(8,128)S(1)} %add.21), channel_id=1, source_target_pairs={{0,4},{1,5},{2,6},{3,7},{4,0},{5,1},{6,2},{7,3},{8,12},{9,13},{10,... | collective-permute-start | bytes 393224 | tf_op jit(solution)/shard_map/ppermute | solution.py:221
  64.6 3.1 %collective-permute-done.6 = f32[128,256]{1,0:T(8,128)S(1)} collective-permute-done((f32[128,256]{1,0:T(8,128)S(1)}, f32[128,256]{1,0:T(8,128)S(1)}, u32[]{:S(2)}, u32[]{:S(2)}) %collective-permute-start.6) | collective-permute-done | bytes 131104 | tf_op jit(solution)/shard_map/ppermute | solution.py:221
  67.7 3.9 %collective-permute-start.7 = (f32[128,256]{1,0:T(8,128)S(1)}, f32[128,256]{1,0:T(8,128)S(1)}, u32[]{:S(2)}, u32[]{:S(2)}) collective-permute-start(f32[128,256]{1,0:T(8,128)S(1)} %add.22), channel_id=1, source_target_pairs={{0,12},{1,13},{2,14},{3,15},{4,8},{5,9},{6,10},{7,11},{8,4},{9,5},... | collective-permute-start | bytes 393224 | tf_op jit(solution)/shard_map/ppermute | solution.py:221
  71.6 3.0 %collective-permute-done.7 = f32[128,256]{1,0:T(8,128)S(1)} collective-permute-done((f32[128,256]{1,0:T(8,128)S(1)}, f32[128,256]{1,0:T(8,128)S(1)}, u32[]{:S(2)}, u32[]{:S(2)}) %collective-permute-start.7) | collective-permute-done | bytes 131104 | tf_op jit(solution)/shard_map/ppermute | solution.py:221
  74.7 0.1 collective-permute-start.8
  74.8 1.3 %collective-permute-done.8.other_ref = f32[128,256]{1,0:T(8,128)S(1)} collective-permute-done((f32[128,256]{1,0:T(8,128)S(1)}, f32[128,256]{1,0:T(8,128)S(1)}, u32[]{:S(2)}, u32[]{:S(2)}) %collective-permute-start.8) | collective-permute-done | bytes 131104 | tf_op jit(solution)/shard_map/ppermute | solution.py:221
  76.1 13.5 %predict.1 = f32[64,512]{1,0:T(8,128)} custom-call(s32[1]{0:T(128)} %bitcast.half_ref, f32[128,256]{1,0:T(8,128)S(1)} %add.23.mine_ref, f32[128,256]{1,0:T(8,128)S(1)} %collective-permute-done.8.other_ref, f32[256,256]{1,0:T(8,128)} %prior_ref.5, f32[256,320]{1,0:T(8,128)} %get-tuple-element.29.region_ref, f32[256,576]{1,0:T(8,128)} %get-tuple-element.30.leaf_ref, ...), custom_call_target="tpu_custom_call" | custom-call | flops 805306368 | bytes 2097152 | tf_op jit(solution)/shard_map/predict/pallas_call | solution.py:292
  (4 shorter events, 0.1 us)
Async XLA Ops:
  18.9 8.3 %copy-start = (f32[128,384]{1,0:T(8,128)S(1)}, f32[128,384]{1,0:T(8,128)}, u32[]{:S(2)}) copy-start(f32[128,384]{1,0:T(8,128)} %get-tuple-element.18.own_ref) | copy-start | bytes 589828
  24.2 26.6 %collective-permute-start.1 = (f32[128,640]{1,0:T(8,128)}, f32[128,640]{1,0:T(8,128)S(1)}, u32[]{:S(2)}, u32[]{:S(2)}) collective-permute-start(f32[128,640]{1,0:T(8,128)} %get-tuple-element.24.own_ref), channel_id=1, source_target_pairs={{0,16},{16,0},{1,17},{17,1},{2,18},{18,2},{3,19},{19,3},{4,20},{20... | collective-permute-start | bytes 983048 | tf_op jit(solution)/shard_map/ppermute | solution.py:221
  27.2 13.0 %collective-permute-start = (f32[128,384]{1,0:T(8,128)S(1)}, f32[128,384]{1,0:T(8,128)S(1)}, u32[]{:S(2)}, u32[]{:S(2)}) collective-permute-start(f32[128,384]{1,0:T(8,128)S(1)} %copy-done), channel_id=1, source_target_pairs={{0,16},{16,0},{1,17},{17,1},{2,18},{18,2},{3,19},{19,3},{4,20},{20... | collective-permute-start | bytes 589832 | tf_op jit(solution)/shard_map/ppermute | solution.py:221
  27.2 1.6 %collective-permute-start.2 = (f32[128,256]{1,0:T(8,128)}, f32[128,256]{1,0:T(8,128)S(1)}, u32[]{:S(2)}, u32[]{:S(2)}) collective-permute-start(f32[128,256]{1,0:T(8,128)} %get-tuple-element.26), channel_id=1, source_target_pairs={{0,1},{1,0},{2,3},{3,2},{4,5},{5,4},{6,7},{7,6},{8,9},{9,8},{10,11... | collective-permute-start | bytes 393224 | tf_op jit(solution)/shard_map/ppermute | solution.py:221
  29.7 21.0 %collective-permute-start.3 = (f32[128,256]{1,0:T(8,128)S(1)}, f32[128,256]{1,0:T(8,128)S(1)}, u32[]{:S(2)}, u32[]{:S(2)}) collective-permute-start(f32[128,256]{1,0:T(8,128)S(1)} %add.18), channel_id=1, source_target_pairs={{0,16},{16,0},{1,17},{17,1},{2,18},{18,2},{3,19},{19,3},{4,20},{20... | collective-permute-start | bytes 393224 | tf_op jit(solution)/shard_map/ppermute | solution.py:221
  54.3 1.6 %collective-permute-start.4 = (f32[128,256]{1,0:T(8,128)}, f32[128,256]{1,0:T(8,128)S(1)}, u32[]{:S(2)}, u32[]{:S(2)}) collective-permute-start(f32[128,256]{1,0:T(8,128)} %get-tuple-element.28), channel_id=1, source_target_pairs={{0,1},{1,0},{2,3},{3,2},{4,5},{5,4},{6,7},{7,6},{8,9},{9,8},{10,11... | collective-permute-start | bytes 393224 | tf_op jit(solution)/shard_map/ppermute | solution.py:221
  56.8 5.9 %collective-permute-start.5 = (f32[128,256]{1,0:T(8,128)S(1)}, f32[128,256]{1,0:T(8,128)S(1)}, u32[]{:S(2)}, u32[]{:S(2)}) collective-permute-start(f32[128,256]{1,0:T(8,128)S(1)} %add.20), channel_id=1, source_target_pairs={{0,2},{1,3},{2,0},{3,1},{4,6},{5,7},{6,4},{7,5},{8,10},{9,11},{10,... | collective-permute-start | bytes 393224 | tf_op jit(solution)/shard_map/ppermute | solution.py:221
  62.7 5.0 %collective-permute-start.6 = (f32[128,256]{1,0:T(8,128)S(1)}, f32[128,256]{1,0:T(8,128)S(1)}, u32[]{:S(2)}, u32[]{:S(2)}) collective-permute-start(f32[128,256]{1,0:T(8,128)S(1)} %add.21), channel_id=1, source_target_pairs={{0,4},{1,5},{2,6},{3,7},{4,0},{5,1},{6,2},{7,3},{8,12},{9,13},{10,... | collective-permute-start | bytes 393224 | tf_op jit(solution)/shard_map/ppermute | solution.py:221
  67.7 7.0 %collective-permute-start.7 = (f32[128,256]{1,0:T(8,128)S(1)}, f32[128,256]{1,0:T(8,128)S(1)}, u32[]{:S(2)}, u32[]{:S(2)}) collective-permute-start(f32[128,256]{1,0:T(8,128)S(1)} %add.22), channel_id=1, source_target_pairs={{0,12},{1,13},{2,14},{3,15},{4,8},{5,9},{6,10},{7,11},{8,4},{9,5},... | collective-permute-start | bytes 393224 | tf_op jit(solution)/shard_map/ppermute | solution.py:221
  74.7 1.4 %collective-permute-start.8 = (f32[128,256]{1,0:T(8,128)S(1)}, f32[128,256]{1,0:T(8,128)S(1)}, u32[]{:S(2)}, u32[]{:S(2)}) collective-permute-start(f32[128,256]{1,0:T(8,128)S(1)} %add.23.mine_ref), channel_id=1, source_target_pairs={{0,1},{1,0},{2,3},{3,2},{4,5},{5,4},{6,7},{7,6},{8,9},{9,8},{10,11... | collective-permute-start | bytes 393224 | tf_op jit(solution)/shard_map/ppermute | solution.py:221

commit v3 on v2

--- a/solution.py
+++ b/solution.py
@@ -22,32 +22,40 @@
     rows = [a[8 * i : 8 * i + 8, :] for i in range(groups)]
     lane = lax.broadcasted_iota(jnp.int32, (8, n), 1)
     sub = lax.broadcasted_iota(jnp.int32, (8, n), 0)
+
+    def col(x, j):
+        return jnp.broadcast_to(x[:, j : j + 1], (8, n))
+
+    def row(x, k):
+        return jnp.take_along_axis(x, jnp.full((8, n), k, jnp.int32), axis=0, mode="promise_in_bounds")
+
     for g in range(groups):
-
-        def col(x, k, g=g):
-            return jnp.broadcast_to(x[:, 8 * g + k : 8 * g + k + 1], (8, n))
-
         p = rows[g]
-        c = [col(p, k) for k in range(8)]
+        c = [col(p, 8 * g + k) for k in range(8)]
+        b = {i: [] for i in range(groups) if i != g}
+        for k in range(8):
+            for i in b:
+                b[i].append(col(rows[i], 8 * g + k))
         inside = (lane >= 8 * g) & (lane < 8 * g + 8)
         p = jnp.where(inside, jnp.where(lane - 8 * g == sub, 1.0, 0.0), p)
+        pivot = row(c[0], 0)
         for k in range(8):
             here = sub == k
-            r = 1.0 / jnp.broadcast_to(c[k][k : k + 1, :], (8, n))
+            r = 1.0 / pivot
             for m in range(k + 1, 8):
-                s = jnp.broadcast_to(c[m][k : k + 1, :], (8, n)) * r
-                c[m] = jnp.where(here, s, c[m] - c[k] * s)
-            s = jnp.broadcast_to(p[k : k + 1, :], (8, n)) * r
+                s = row(c[m], k) * r
+                left = c[m] - c[k] * s
+                if m == k + 1:
+                    pivot = row(left, m)
+                c[m] = jnp.where(here, s, left)
+            s = row(p, k) * r
             p = jnp.where(here, s, p - c[k] * s)
-        pr = [jnp.broadcast_to(p[k : k + 1, :], (8, n)) for k in range(8)]
-        for i in range(groups):
-            if i == g:
-                continue
-            old = rows[i]
-            t = [col(old, k) * pr[k] for k in range(8)]
+        pr = [row(p, k) for k in range(8)]
+        for i in b:
+            t = [b[i][k] * pr[k] for k in range(8)]
             while len(t) > 1:
                 t = [t[q] + t[q + 1] for q in range(0, len(t), 2)]
-            rows[i] = jnp.where(inside, 0.0, old) - t[0]
+            rows[i] = jnp.where(inside, 0.0, rows[i]) - t[0]
         rows[g] = p
     return jnp.concatenate(rows, axis=0)
 
@@ -169,7 +177,7 @@
         factor_ref[i] = factor[i]
 
 
-def region_kernel(half_ref, factor_ref, own_ref, other_ref, upper_ref, solved_ref, keep_ref, send_ref, pieces):
+def region_kernel(half_ref, factor_ref, own_ref, other_ref, solved_ref, keep_ref, send_ref, pieces):
     h = own_ref.shape[0]
     r = 2 * h
     rows = own_ref[...] + other_ref[...]
@@ -179,13 +187,20 @@
     x = spd_apply((factor_ref[0], factor_ref[1], factor_ref[2]), jnp.concatenate([cross, y], axis=1))
     solved_ref[...] = x
     pieces[0], pieces[1] = pack_halves(-mm(cross, x, 0, 0))
-    keep_ref[...] = upper_ref[...] + pieces[half_ref[0]]
+    keep_ref[...] = pieces[half_ref[0]]
     send_ref[...] = pieces[1 - half_ref[0]]
 
 
-def global_kernel(half_ref, mine_ref, other_ref, prior_ref, region_ref, leaf_ref, table_ref, out_ref, pieces):
-    r = prior_ref.shape[0]
-    h = r // 2
+def combine_kernel(region_ref, leaf_ref, table_ref, slope_ref, base_ref):
+    r = region_ref.shape[0]
+    leaf_table = table_ref[2 * r :, :]
+    upper = table_ref[: 2 * r, :] - mm(leaf_ref[:, : 2 * r], leaf_table, 0, 0)
+    slope_ref[...] = upper[:r] - mm(region_ref[:, :r], upper[r:], 0, 0)
+    base_ref[...] = mm(region_ref[:, r:], upper[r:], 0, 0) + mm(leaf_ref[:, 2 * r :], leaf_table, 0, 0)
+
+
+def global_kernel(half_ref, mine_ref, other_ref, prior_ref, slope_ref, base_ref, out_ref, pieces):
+    h = mine_ref.shape[0]
     q = h // 2
     pieces[half_ref[0]] = mine_ref[...]
     pieces[1 - half_ref[0]] = other_ref[...]
@@ -195,9 +210,7 @@
     low = jnp.concatenate([jnp.zeros_like(b[:, :h]), b[:, :h]], axis=1)
     y = jnp.concatenate([a[:, h + q :], b[:, h + q :]], axis=0)
     w_g = spd_apply(spd_factor(prior_ref[...] + jnp.concatenate([top, low], axis=0)), y)
-    w_r = region_ref[:, r:] - mm(region_ref[:, :r], w_g)
-    w_l = leaf_ref[:, 2 * r :] - mm(leaf_ref[:, : 2 * r], jnp.concatenate([w_g, w_r], axis=0))
-    out_ref[...] = mm(jnp.concatenate([w_g, w_r, w_l], axis=0), table_ref[...], 0, 0)
+    out_ref[...] = base_ref[...] + mm(w_g, slope_ref[...], 0, 0)
 
 
 SMEM = pl.BlockSpec(memory_space=pltpu.SMEM)
@@ -273,31 +286,39 @@
         cost_estimate=cost(8 * r * r * r, r),
     )(own, in_vmem(other), region_prior, table)
     own, other = swap_halfway(cross, "region", n_region)
-    upper = keep + swap(send, "super", n_super, 1)
-    for mask in masks(n_region, 0):
-        upper = upper + swap(upper, "region", n_region, mask)
+    moved = swap(send, "super", n_super, 1)
+    upper, upper_moved = swap_halfway(keep + moved, "region", n_region)
     region_solved, keep, send = pl.pallas_call(
         region_kernel,
         out_shape=(shape(r, r + fields), shape(h, r), shape(h, r)),
-        in_specs=[SMEM] + [VMEM] * 4,
+        in_specs=[SMEM] + [VMEM] * 3,
         out_specs=(VMEM,) * 3,
         scratch_shapes=[pieces],
         name="region",
         cost_estimate=cost(4 * r * r * (r + fields), r),
-    )(half, region_factor, own, in_vmem(other), in_vmem(upper))
-    mine = keep + swap(send, "super", n_super, 1)
+    )(half, region_factor, own, in_vmem(other))
+    mine = keep + upper + upper_moved + swap(send, "super", n_super, 1)
+    slope, base = pl.pallas_call(
+        combine_kernel,
+        out_shape=(shape(r, nsite), shape(fields, nsite)),
+        in_specs=[VMEM] * 3,
+        out_specs=(VMEM,) * 2,
+        name="combine",
+        cost_estimate=cost(6 * r * r * nsite, 0),
+    )(region_solved, solved, table)
     for mask in masks(n_super, 1):
-        mine = mine + swap(mine, "super", n_super, mask)
+        moved = swap(mine, "super", n_super, mask)
+        mine = mine + moved
     other = swap(mine, "super", n_super, 1)
     return pl.pallas_call(
         global_kernel,
         out_shape=shape(fields, nsite),
-        in_specs=[SMEM] + [VMEM] * 6,
+        in_specs=[SMEM] + [VMEM] * 5,
         out_specs=VMEM,
         scratch_shapes=[pieces],
         name="predict",
         cost_estimate=cost(8 * r * r * r, r),
-    )(half, in_vmem(mine), in_vmem(other), global_prior, region_solved, solved, table)
+    )(half, in_vmem(mine), in_vmem(other), global_prior, slope, base)
 
 
 def solution(mesh):

time: 89.9 us -> 88.1 us (0.980)
  waiting for transfers between devices: 22.9 us -> 21.5 us
    pallas_call x0 -> x1, Pallas kernels: none -> 4.58 us  [shards(): pl.pallas_call(combine_kernel, out_shape=(shape(r, nsite), shape(fields,...]
    pallas_call x1, Pallas kernels: 13.5 us -> 10.7 us  [shards(): pl.pallas_call(global_kernel, out_shape=shape(fields, nsite), in_specs=[S...]
    ppermute x9, waiting for transfers between devices: 22.9 us -> 21.5 us  [swap(): return lax.ppermute(x, axis, [(i, i ^ mask) for i in range(size)])]
    pallas_call x1, Pallas kernels: 10.6 us -> 9.46 us  [shards(): pl.pallas_call(region_factor_kernel, out_shape=shape(3, h, h), in_specs=[...]
    pallas_call x1, Pallas kernels: 18.9 us -> 17.8 us  [shards(): pl.pallas_call(functools.partial(leaf_kernel, nobs // width), out_shape=(...]
    add x6 -> x5, other arithmetic: 1.91 us -> 1.91 us  [the longest x1 0.94 us: shards(): mine = keep + upper + upper_moved + swap(send, 'super', n_super, 1)]
  transfers between devices with their start and end apart: 9 -> 9, of which waited for: 7 -> 6; matrix products, arithmetic and copies ran while one was open for 1% -> 1% of each run, Pallas kernels for 12% -> 20%
where the time goes in v3:
time: 88.1 us; the launch traced here: 87.8 us
  Pallas kernels  51.3 us (58%)
  waiting for transfers between devices  21.5 us (24%)
  starting transfers between devices  13 us (15%)
  other arithmetic  1.91 us (2%)
    ppermute x9, waiting for transfers between devices, swap(): return lax.ppermute(x, axis, [(i, i ^ mask) for i in range(size)])  21.5 us
    pallas_call x1, Pallas kernels, shards(): pl.pallas_call(functools.partial(leaf_kernel, nobs // width), out_shape=(...  17.8 us
    ppermute x9, starting transfers between devices, swap(): return lax.ppermute(x, axis, [(i, i ^ mask) for i in range(size)])  13 us
    pallas_call x1, Pallas kernels, shards(): pl.pallas_call(global_kernel, out_shape=shape(fields, nsite), in_specs=[S...  10.7 us
    pallas_call x1, Pallas kernels, shards(): pl.pallas_call(region_factor_kernel, out_shape=shape(3, h, h), in_specs=[...  9.46 us
    pallas_call x1, Pallas kernels, shards(): pl.pallas_call(leaf_rest_kernel, out_shape=(shape(r, 2 * r + fields), sha...  5.3 us
    pallas_call x1, Pallas kernels, shards(): pl.pallas_call(combine_kernel, out_shape=(shape(r, nsite), shape(fields,...  4.58 us
    pallas_call x1, Pallas kernels, shards(): pl.pallas_call(region_kernel, out_shape=(shape(r, r + fields), shape(h, r...  3.49 us
  transfers between devices with their start and end apart: 9, of which 6 were waited for; matrix products, arithmetic and copies ran while one was open for 1% of the time, Pallas kernels for 20%

profile of v3, /device:TPU:0, one launch (start us, length us, event | category | flops | bytes accessed | tf_op | source)
XLA Modules:
  0.0 87.8 jit_solution(12823036361198782355)
XLA Ops:
  0.0 17.8 %leaf.1 = (f32[128,384]{1,0:T(8,128)}, f32[3,128,128]{2,1,0:T(8,128)}, f32[832,256]{1,0:T(8,128)}, f32[576,256]{1,0:T(8,128)}, f32[320,256]{1,0:T(8,128)}) custom-call(f32[3]{0:T(128)} %scale_ref.3, f32[2,256]{1,0:T(2,128)} %kg_ref.3, f32[1,2,256]{2,1,0:T(2,128)} %kr_ref.3, f32[1,2,256]{2,1,0:T(2,128)} %kl_ref.3, f32[2,4096]{1,0:T(2,128)} %coords_ref.1, ...), custom_call_target="tpu_custom_call" | custom-call | flops 34024194048 | bytes 2097152 | tf_op jit(solution)/shard_map/leaf/pallas_call | solution.py:260
  17.8 0.0 copy-start
  17.8 5.3 %leaf_rest.1 = (f32[256,576]{1,0:T(8,128)}, f32[128,640]{1,0:T(8,128)}, f32[128,256]{1,0:T(8,128)}, f32[128,256]{1,0:T(8,128)}, f32[768,512]{1,0:T(8,128)}) custom-call(s32[1]{0:T(128)} %bitcast.half_ref, f32[3]{0:T(128)} %scale_ref.3, f32[2,256]{1,0:T(2,128)} %kg_ref.3, f32[1,2,256]{2,1,0:T(2,128)} %kr_ref.3, f32[1,2,256]{2,1,0:T(2,128)} %kl_ref.3, ...), custom_call_target="tpu_custom_call" | custom-call | flops 956301312 | bytes 2097152 | tf_op jit(solution)/shard_map/leaf_rest/pallas_call | solution.py:271
  23.1 3.0 %collective-permute-start.1 = (f32[128,640]{1,0:T(8,128)}, f32[128,640]{1,0:T(8,128)S(1)}, u32[]{:S(2)}, u32[]{:S(2)}) collective-permute-start(f32[128,640]{1,0:T(8,128)} %get-tuple-element.26.own_ref), channel_id=1, source_target_pairs={{0,16},{16,0},{1,17},{17,1},{2,18},{18,2},{3,19},{19,3},{4,20},{20... | collective-permute-start | bytes 983048 | tf_op jit(solution)/shard_map/ppermute | solution.py:234
  26.1 0.0 copy-done
  26.1 0.1 collective-permute-start
  26.2 0.0 collective-permute-start.2
  26.2 1.6 %collective-permute-done.2 = f32[128,256]{1,0:T(8,128)S(1)} collective-permute-done((f32[128,256]{1,0:T(8,128)}, f32[128,256]{1,0:T(8,128)S(1)}, u32[]{:S(2)}, u32[]{:S(2)}) %collective-permute-start.2) | collective-permute-done | bytes 131104 | tf_op jit(solution)/shard_map/ppermute | solution.py:234
  27.7 0.9 %add.21 = f32[128,256]{1,0:T(8,128)S(1)} add(f32[128,256]{1,0:T(8,128)} %get-tuple-element.28, f32[128,256]{1,0:T(8,128)S(1)} %collective-permute-done.2) | non-fusion elementwise | flops 32768 | bytes 393216 | tf_op jit(solution)/shard_map/add | solution.py:290
  28.6 2.0 %collective-permute-start.3 = (f32[128,256]{1,0:T(8,128)S(1)}, f32[128,256]{1,0:T(8,128)S(1)}, u32[]{:S(2)}, u32[]{:S(2)}) collective-permute-start(f32[128,256]{1,0:T(8,128)S(1)} %add.21), channel_id=1, source_target_pairs={{0,16},{16,0},{1,17},{17,1},{2,18},{18,2},{3,19},{19,3},{4,20},{20... | collective-permute-start | bytes 393224 | tf_op jit(solution)/shard_map/ppermute | solution.py:234
  30.6 8.4 %collective-permute-done.other_ref = f32[128,384]{1,0:T(8,128)S(1)} collective-permute-done((f32[128,384]{1,0:T(8,128)S(1)}, f32[128,384]{1,0:T(8,128)S(1)}, u32[]{:S(2)}, u32[]{:S(2)}) %collective-permute-start) | collective-permute-done | bytes 196640 | tf_op jit(solution)/shard_map/ppermute | solution.py:234
  39.1 9.5 %region_factor.1.factor_ref = f32[3,128,128]{2,1,0:T(8,128)} custom-call(f32[128,384]{1,0:T(8,128)} %get-tuple-element.20.own_ref, f32[128,384]{1,0:T(8,128)S(1)} %collective-permute-done.other_ref, f32[1,256,256]{2,1,0:T(8,128)} %prior_ref.4, f32[768,512]{1,0:T(8,128)} %get-tuple-element.25.after_ref.table_ref), custom_call_target="tpu_custom_call" | custom-call | flops 805306368 | bytes 2097152 | tf_op jit(solution)/shard_map/region_factor/pallas_call | solution.py:280
  48.5 0.0 collective-permute-done.1.other_ref
  48.5 3.5 %region.1 = (f32[256,320]{1,0:T(8,128)}, f32[128,256]{1,0:T(8,128)}, f32[128,256]{1,0:T(8,128)}) custom-call(s32[1]{0:T(128)} %bitcast.half_ref, f32[3,128,128]{2,1,0:T(8,128)} %region_factor.1.factor_ref, f32[128,640]{1,0:T(8,128)} %get-tuple-element.26.own_ref, f32[128,640]{1,0:T(8,128)S(1)} %collective-permute-done.1.other_ref), custom_call_target="tpu_custom_call" | custom-call | flops 503316480 | bytes 2097152 | tf_op jit(solution)/shard_map/region/pallas_call | solution.py:291
  52.0 0.0 collective-permute-start.4
  52.0 0.0 collective-permute-done.3
  52.0 1.6 %collective-permute-done.4 = f32[128,256]{1,0:T(8,128)S(1)} collective-permute-done((f32[128,256]{1,0:T(8,128)}, f32[128,256]{1,0:T(8,128)S(1)}, u32[]{:S(2)}, u32[]{:S(2)}) %collective-permute-start.4) | collective-permute-done | bytes 131104 | tf_op jit(solution)/shard_map/ppermute | solution.py:234
  53.6 0.9 %add_add_fusion = f32[128,256]{1,0:T(8,128)S(1)} fusion(f32[128,256]{1,0:T(8,128)S(1)} %collective-permute-done.4, f32[128,256]{1,0:T(8,128)S(1)} %collective-permute-done.3, f32[128,256]{1,0:T(8,128)} %get-tuple-element.27, f32[128,256]{1,0:T(8,128)S(1)} %add.21), kind=kLoop, calls=%fused_computation | loop fusion | flops 98304 | bytes 655360 | tf_op jit(solution)/shard_map/add | solution.py:300
  54.5 2.1 %collective-permute-start.5 = (f32[128,256]{1,0:T(8,128)S(1)}, f32[128,256]{1,0:T(8,128)S(1)}, u32[]{:S(2)}, u32[]{:S(2)}) collective-permute-start(f32[128,256]{1,0:T(8,128)S(1)} %add_add_fusion), channel_id=1, source_target_pairs={{0,2},{1,3},{2,0},{3,1},{4,6},{5,7},{6,4},{7,5},{8,10},{9,11},{10,... | collective-permute-start | bytes 393224 | tf_op jit(solution)/shard_map/ppermute | solution.py:234
  56.6 3.8 %collective-permute-done.5 = f32[128,256]{1,0:T(8,128)S(1)} collective-permute-done((f32[128,256]{1,0:T(8,128)S(1)}, f32[128,256]{1,0:T(8,128)S(1)}, u32[]{:S(2)}, u32[]{:S(2)}) %collective-permute-start.5) | collective-permute-done | bytes 131104 | tf_op jit(solution)/shard_map/ppermute | solution.py:234
  60.4 1.9 %collective-permute-start.6 = (f32[128,256]{1,0:T(8,128)S(1)}, f32[128,256]{1,0:T(8,128)S(1)}, u32[]{:S(2)}, u32[]{:S(2)}) collective-permute-start(f32[128,256]{1,0:T(8,128)S(1)} %add.25), channel_id=1, source_target_pairs={{0,4},{1,5},{2,6},{3,7},{4,0},{5,1},{6,2},{7,3},{8,12},{9,13},{10,... | collective-permute-start | bytes 393224 | tf_op jit(solution)/shard_map/ppermute | solution.py:234
  62.3 3.1 %collective-permute-done.6 = f32[128,256]{1,0:T(8,128)S(1)} collective-permute-done((f32[128,256]{1,0:T(8,128)S(1)}, f32[128,256]{1,0:T(8,128)S(1)}, u32[]{:S(2)}, u32[]{:S(2)}) %collective-permute-start.6) | collective-permute-done | bytes 131104 | tf_op jit(solution)/shard_map/ppermute | solution.py:234
  65.5 3.9 %collective-permute-start.7 = (f32[128,256]{1,0:T(8,128)S(1)}, f32[128,256]{1,0:T(8,128)S(1)}, u32[]{:S(2)}, u32[]{:S(2)}) collective-permute-start(f32[128,256]{1,0:T(8,128)S(1)} %add.26), channel_id=1, source_target_pairs={{0,12},{1,13},{2,14},{3,15},{4,8},{5,9},{6,10},{7,11},{8,4},{9,5},... | collective-permute-start | bytes 393224 | tf_op jit(solution)/shard_map/ppermute | solution.py:234
  69.4 3.1 %collective-permute-done.7 = f32[128,256]{1,0:T(8,128)S(1)} collective-permute-done((f32[128,256]{1,0:T(8,128)S(1)}, f32[128,256]{1,0:T(8,128)S(1)}, u32[]{:S(2)}, u32[]{:S(2)}) %collective-permute-start.7) | collective-permute-done | bytes 131104 | tf_op jit(solution)/shard_map/ppermute | solution.py:234
  72.4 0.1 collective-permute-start.8
  72.5 4.6 %combine.1 = (f32[256,512]{1,0:T(8,128)}, f32[64,512]{1,0:T(8,128)}) custom-call(f32[256,320]{1,0:T(8,128)} %get-tuple-element.31.region_ref, f32[256,576]{1,0:T(8,128)} %get-tuple-element.32.leaf_ref, f32[768,512]{1,0:T(8,128)} %get-tuple-element.25.after_ref.table_ref), custom_call_target="tpu_custom_call" | custom-call | flops 1207959552 | bytes 2097152 | tf_op jit(solution)/shard_map/combine/pallas_call | solution.py:301
  77.1 0.0 collective-permute-done.8.other_ref
  77.1 10.7 %predict.1 = f32[64,512]{1,0:T(8,128)} custom-call(s32[1]{0:T(128)} %bitcast.half_ref, f32[128,256]{1,0:T(8,128)S(1)} %add.27.mine_ref, f32[128,256]{1,0:T(8,128)S(1)} %collective-permute-done.8.other_ref, f32[256,256]{1,0:T(8,128)} %prior_ref.5, f32[256,512]{1,0:T(8,128)} %get-tuple-element.33.slope_ref, f32[64,512]{1,0:T(8,128)} %get-tuple-element.34.base_ref), custom_call_target="tpu_custom_call" | custom-call | flops 805306368 | bytes 2097152 | tf_op jit(solution)/shard_map/predict/pallas_call | solution.py:313
  (3 shorter events, 0.1 us)
Async XLA Ops:
  17.8 8.3 %copy-start = (f32[128,384]{1,0:T(8,128)S(1)}, f32[128,384]{1,0:T(8,128)}, u32[]{:S(2)}) copy-start(f32[128,384]{1,0:T(8,128)} %get-tuple-element.20.own_ref) | copy-start | bytes 589828
  23.1 25.5 %collective-permute-start.1 = (f32[128,640]{1,0:T(8,128)}, f32[128,640]{1,0:T(8,128)S(1)}, u32[]{:S(2)}, u32[]{:S(2)}) collective-permute-start(f32[128,640]{1,0:T(8,128)} %get-tuple-element.26.own_ref), channel_id=1, source_target_pairs={{0,16},{16,0},{1,17},{17,1},{2,18},{18,2},{3,19},{19,3},{4,20},{20... | collective-permute-start | bytes 983048 | tf_op jit(solution)/shard_map/ppermute | solution.py:234
  26.1 13.0 %collective-permute-start = (f32[128,384]{1,0:T(8,128)S(1)}, f32[128,384]{1,0:T(8,128)S(1)}, u32[]{:S(2)}, u32[]{:S(2)}) collective-permute-start(f32[128,384]{1,0:T(8,128)S(1)} %copy-done), channel_id=1, source_target_pairs={{0,16},{16,0},{1,17},{17,1},{2,18},{18,2},{3,19},{19,3},{4,20},{20... | collective-permute-start | bytes 589832 | tf_op jit(solution)/shard_map/ppermute | solution.py:234
  26.2 1.6 %collective-permute-start.2 = (f32[128,256]{1,0:T(8,128)}, f32[128,256]{1,0:T(8,128)S(1)}, u32[]{:S(2)}, u32[]{:S(2)}) collective-permute-start(f32[128,256]{1,0:T(8,128)} %get-tuple-element.29), channel_id=1, source_target_pairs={{0,1},{1,0},{2,3},{3,2},{4,5},{5,4},{6,7},{7,6},{8,9},{9,8},{10,11... | collective-permute-start | bytes 393224 | tf_op jit(solution)/shard_map/ppermute | solution.py:234
  28.6 23.4 %collective-permute-start.3 = (f32[128,256]{1,0:T(8,128)S(1)}, f32[128,256]{1,0:T(8,128)S(1)}, u32[]{:S(2)}, u32[]{:S(2)}) collective-permute-start(f32[128,256]{1,0:T(8,128)S(1)} %add.21), channel_id=1, source_target_pairs={{0,16},{16,0},{1,17},{17,1},{2,18},{18,2},{3,19},{19,3},{4,20},{20... | collective-permute-start | bytes 393224 | tf_op jit(solution)/shard_map/ppermute | solution.py:234
  52.0 1.6 %collective-permute-start.4 = (f32[128,256]{1,0:T(8,128)}, f32[128,256]{1,0:T(8,128)S(1)}, u32[]{:S(2)}, u32[]{:S(2)}) collective-permute-start(f32[128,256]{1,0:T(8,128)} %get-tuple-element.30), channel_id=1, source_target_pairs={{0,1},{1,0},{2,3},{3,2},{4,5},{5,4},{6,7},{7,6},{8,9},{9,8},{10,11... | collective-permute-start | bytes 393224 | tf_op jit(solution)/shard_map/ppermute | solution.py:234
  54.5 5.9 %collective-permute-start.5 = (f32[128,256]{1,0:T(8,128)S(1)}, f32[128,256]{1,0:T(8,128)S(1)}, u32[]{:S(2)}, u32[]{:S(2)}) collective-permute-start(f32[128,256]{1,0:T(8,128)S(1)} %add_add_fusion), channel_id=1, source_target_pairs={{0,2},{1,3},{2,0},{3,1},{4,6},{5,7},{6,4},{7,5},{8,10},{9,11},{10,... | collective-permute-start | bytes 393224 | tf_op jit(solution)/shard_map/ppermute | solution.py:234
  60.4 5.0 %collective-permute-start.6 = (f32[128,256]{1,0:T(8,128)S(1)}, f32[128,256]{1,0:T(8,128)S(1)}, u32[]{:S(2)}, u32[]{:S(2)}) collective-permute-start(f32[128,256]{1,0:T(8,128)S(1)} %add.25), channel_id=1, source_target_pairs={{0,4},{1,5},{2,6},{3,7},{4,0},{5,1},{6,2},{7,3},{8,12},{9,13},{10,... | collective-permute-start | bytes 393224 | tf_op jit(solution)/shard_map/ppermute | solution.py:234
  65.5 7.0 %collective-permute-start.7 = (f32[128,256]{1,0:T(8,128)S(1)}, f32[128,256]{1,0:T(8,128)S(1)}, u32[]{:S(2)}, u32[]{:S(2)}) collective-permute-start(f32[128,256]{1,0:T(8,128)S(1)} %add.26), channel_id=1, source_target_pairs={{0,12},{1,13},{2,14},{3,15},{4,8},{5,9},{6,10},{7,11},{8,4},{9,5},... | collective-permute-start | bytes 393224 | tf_op jit(solution)/shard_map/ppermute | solution.py:234
  72.4 4.7 %collective-permute-start.8 = (f32[128,256]{1,0:T(8,128)S(1)}, f32[128,256]{1,0:T(8,128)S(1)}, u32[]{:S(2)}, u32[]{:S(2)}) collective-permute-start(f32[128,256]{1,0:T(8,128)S(1)} %add.27.mine_ref), channel_id=1, source_target_pairs={{0,1},{1,0},{2,3},{3,2},{4,5},{5,4},{6,7},{7,6},{8,9},{9,8},{10,11... | collective-permute-start | bytes 393224 | tf_op jit(solution)/shard_map/ppermute | solution.py:234

commit v4 on v3

--- a/solution.py
+++ b/solution.py
@@ -191,12 +191,18 @@
     send_ref[...] = pieces[1 - half_ref[0]]
 
 
-def combine_kernel(region_ref, leaf_ref, table_ref, slope_ref, base_ref):
+def combine_leaf_kernel(leaf_ref, table_ref, upper_ref, base_ref):
+    r = leaf_ref.shape[0]
+    leaf_table = table_ref[2 * r :, :]
+    upper_ref[...] = table_ref[: 2 * r, :] - mm(leaf_ref[:, : 2 * r], leaf_table, 0, 0)
+    base_ref[...] = mm(leaf_ref[:, 2 * r :], leaf_table, 0, 0)
+
+
+def combine_region_kernel(region_ref, upper_ref, leaf_base_ref, slope_ref, base_ref):
     r = region_ref.shape[0]
-    leaf_table = table_ref[2 * r :, :]
-    upper = table_ref[: 2 * r, :] - mm(leaf_ref[:, : 2 * r], leaf_table, 0, 0)
-    slope_ref[...] = upper[:r] - mm(region_ref[:, :r], upper[r:], 0, 0)
-    base_ref[...] = mm(region_ref[:, r:], upper[r:], 0, 0) + mm(leaf_ref[:, 2 * r :], leaf_table, 0, 0)
+    region_table = upper_ref[r:, :]
+    slope_ref[...] = upper_ref[:r, :] - mm(region_ref[:, :r], region_table, 0, 0)
+    base_ref[...] = leaf_base_ref[...] + mm(region_ref[:, r:], region_table, 0, 0)
 
 
 def global_kernel(half_ref, mine_ref, other_ref, prior_ref, slope_ref, base_ref, out_ref, pieces):
@@ -298,14 +304,22 @@
         cost_estimate=cost(4 * r * r * (r + fields), r),
     )(half, region_factor, own, in_vmem(other))
     mine = keep + upper + upper_moved + swap(send, "super", n_super, 1)
+    upper_table, leaf_base = pl.pallas_call(
+        combine_leaf_kernel,
+        out_shape=(shape(2 * r, nsite), shape(fields, nsite)),
+        in_specs=[VMEM] * 2,
+        out_specs=(VMEM,) * 2,
+        name="combine_leaf",
+        cost_estimate=cost(4 * r * r * nsite, 0),
+    )(solved, table)
     slope, base = pl.pallas_call(
-        combine_kernel,
+        combine_region_kernel,
         out_shape=(shape(r, nsite), shape(fields, nsite)),
         in_specs=[VMEM] * 3,
         out_specs=(VMEM,) * 2,
-        name="combine",
-        cost_estimate=cost(6 * r * r * nsite, 0),
-    )(region_solved, solved, table)
+        name="combine_region",
+        cost_estimate=cost(2 * r * r * nsite, 0),
+    )(region_solved, upper_table, leaf_base)
     for mask in masks(n_super, 1):
         moved = swap(mine, "super", n_super, mask)
         mine = mine + moved

time: 88.1 us -> 90.2 us (1.024)
  Pallas kernels: 51.3 us -> 53.3 us
    pallas_call x1 -> x2, Pallas kernels: 4.58 us -> 6.56 us  [the longest x1 3.69 us: shards(): pl.pallas_call(combine_leaf_kernel, out_shape=(shape(2 * r, nsite), shape...]
  transfers between devices with their start and end apart: 9 -> 9, of which waited for: 6 -> 6; matrix products, arithmetic and copies ran while one was open for 1% -> 1% of each run, Pallas kernels for 20% -> 22%
where the time goes in v4:
time: 90.2 us; the launch traced here: 89.8 us
  Pallas kernels  53.3 us (59%)
  waiting for transfers between devices  21.5 us (24%)
  starting transfers between devices  13 us (14%)
  other arithmetic  1.91 us (2%)
    ppermute x9, waiting for transfers between devices, swap(): return lax.ppermute(x, axis, [(i, i ^ mask) for i in range(size)])  21.5 us
    pallas_call x1, Pallas kernels, shards(): pl.pallas_call(functools.partial(leaf_kernel, nobs // width), out_shape=(...  17.8 us
    ppermute x9, starting transfers between devices, swap(): return lax.ppermute(x, axis, [(i, i ^ mask) for i in range(size)])  13 us
    pallas_call x1, Pallas kernels, shards(): pl.pallas_call(global_kernel, out_shape=shape(fields, nsite), in_specs=[S...  10.7 us
    pallas_call x1, Pallas kernels, shards(): pl.pallas_call(region_factor_kernel, out_shape=shape(3, h, h), in_specs=[...  9.49 us
    pallas_call x1, Pallas kernels, shards(): pl.pallas_call(leaf_rest_kernel, out_shape=(shape(r, 2 * r + fields), sha...  5.3 us
    pallas_call x1, Pallas kernels, shards(): pl.pallas_call(combine_leaf_kernel, out_shape=(shape(2 * r, nsite), shape...  3.69 us
    pallas_call x1, Pallas kernels, shards(): pl.pallas_call(region_kernel, out_shape=(shape(r, r + fields), shape(h, r...  3.49 us
  transfers between devices with their start and end apart: 9, of which 6 were waited for; matrix products, arithmetic and copies ran while one was open for 1% of the time, Pallas kernels for 22%

profile of v4, /device:TPU:0, one launch (start us, length us, event | category | flops | bytes accessed | tf_op | source)
XLA Modules:
  0.0 89.8 jit_solution(1456390999034149686)
XLA Ops:
  0.0 17.8 %leaf.1 = (f32[128,384]{1,0:T(8,128)}, f32[3,128,128]{2,1,0:T(8,128)}, f32[832,256]{1,0:T(8,128)}, f32[576,256]{1,0:T(8,128)}, f32[320,256]{1,0:T(8,128)}) custom-call(f32[3]{0:T(128)} %scale_ref.3, f32[2,256]{1,0:T(2,128)} %kg_ref.3, f32[1,2,256]{2,1,0:T(2,128)} %kr_ref.3, f32[1,2,256]{2,1,0:T(2,128)} %kl_ref.3, f32[2,4096]{1,0:T(2,128)} %coords_ref.1, ...), custom_call_target="tpu_custom_call" | custom-call | flops 34024194048 | bytes 2097152 | tf_op jit(solution)/shard_map/leaf/pallas_call | solution.py:266
  17.8 0.0 copy-start
  17.8 5.3 %leaf_rest.1 = (f32[256,576]{1,0:T(8,128)}, f32[128,640]{1,0:T(8,128)}, f32[128,256]{1,0:T(8,128)}, f32[128,256]{1,0:T(8,128)}, f32[768,512]{1,0:T(8,128)}) custom-call(s32[1]{0:T(128)} %bitcast.half_ref, f32[3]{0:T(128)} %scale_ref.3, f32[2,256]{1,0:T(2,128)} %kg_ref.3, f32[1,2,256]{2,1,0:T(2,128)} %kr_ref.3, f32[1,2,256]{2,1,0:T(2,128)} %kl_ref.3, ...), custom_call_target="tpu_custom_call" | custom-call | flops 956301312 | bytes 2097152 | tf_op jit(solution)/shard_map/leaf_rest/pallas_call | solution.py:277
  23.1 3.0 %collective-permute-start.1 = (f32[128,640]{1,0:T(8,128)}, f32[128,640]{1,0:T(8,128)S(1)}, u32[]{:S(2)}, u32[]{:S(2)}) collective-permute-start(f32[128,640]{1,0:T(8,128)} %get-tuple-element.28.own_ref), channel_id=1, source_target_pairs={{0,16},{16,0},{1,17},{17,1},{2,18},{18,2},{3,19},{19,3},{4,20},{20... | collective-permute-start | bytes 983048 | tf_op jit(solution)/shard_map/ppermute | solution.py:240
  26.1 0.0 copy-done
  26.1 0.1 collective-permute-start
  26.2 0.0 collective-permute-start.2
  26.2 1.6 %collective-permute-done.2 = f32[128,256]{1,0:T(8,128)S(1)} collective-permute-done((f32[128,256]{1,0:T(8,128)}, f32[128,256]{1,0:T(8,128)S(1)}, u32[]{:S(2)}, u32[]{:S(2)}) %collective-permute-start.2) | collective-permute-done | bytes 131104 | tf_op jit(solution)/shard_map/ppermute | solution.py:240
  27.7 0.9 %add.21 = f32[128,256]{1,0:T(8,128)S(1)} add(f32[128,256]{1,0:T(8,128)} %get-tuple-element.30, f32[128,256]{1,0:T(8,128)S(1)} %collective-permute-done.2) | non-fusion elementwise | flops 32768 | bytes 393216 | tf_op jit(solution)/shard_map/add | solution.py:296
  28.6 2.0 %collective-permute-start.3 = (f32[128,256]{1,0:T(8,128)S(1)}, f32[128,256]{1,0:T(8,128)S(1)}, u32[]{:S(2)}, u32[]{:S(2)}) collective-permute-start(f32[128,256]{1,0:T(8,128)S(1)} %add.21), channel_id=1, source_target_pairs={{0,16},{16,0},{1,17},{17,1},{2,18},{18,2},{3,19},{19,3},{4,20},{20... | collective-permute-start | bytes 393224 | tf_op jit(solution)/shard_map/ppermute | solution.py:240
  30.6 8.4 %collective-permute-done.other_ref = f32[128,384]{1,0:T(8,128)S(1)} collective-permute-done((f32[128,384]{1,0:T(8,128)S(1)}, f32[128,384]{1,0:T(8,128)S(1)}, u32[]{:S(2)}, u32[]{:S(2)}) %collective-permute-start) | collective-permute-done | bytes 196640 | tf_op jit(solution)/shard_map/ppermute | solution.py:240
  39.1 9.5 %region_factor.1.factor_ref = f32[3,128,128]{2,1,0:T(8,128)} custom-call(f32[128,384]{1,0:T(8,128)} %get-tuple-element.22.own_ref, f32[128,384]{1,0:T(8,128)S(1)} %collective-permute-done.other_ref, f32[1,256,256]{2,1,0:T(8,128)} %prior_ref.4, f32[768,512]{1,0:T(8,128)} %get-tuple-element.27.after_ref.table_ref), custom_call_target="tpu_custom_call" | custom-call | flops 805306368 | bytes 2097152 | tf_op jit(solution)/shard_map/region_factor/pallas_call | solution.py:286
  48.5 0.0 collective-permute-done.1.other_ref
  48.5 3.5 %region.1 = (f32[256,320]{1,0:T(8,128)}, f32[128,256]{1,0:T(8,128)}, f32[128,256]{1,0:T(8,128)}) custom-call(s32[1]{0:T(128)} %bitcast.half_ref, f32[3,128,128]{2,1,0:T(8,128)} %region_factor.1.factor_ref, f32[128,640]{1,0:T(8,128)} %get-tuple-element.28.own_ref, f32[128,640]{1,0:T(8,128)S(1)} %collective-permute-done.1.other_ref), custom_call_target="tpu_custom_call" | custom-call | flops 503316480 | bytes 2097152 | tf_op jit(solution)/shard_map/region/pallas_call | solution.py:297
  52.0 0.0 collective-permute-start.4
  52.0 0.0 collective-permute-done.3
  52.0 1.6 %collective-permute-done.4 = f32[128,256]{1,0:T(8,128)S(1)} collective-permute-done((f32[128,256]{1,0:T(8,128)}, f32[128,256]{1,0:T(8,128)S(1)}, u32[]{:S(2)}, u32[]{:S(2)}) %collective-permute-start.4) | collective-permute-done | bytes 131104 | tf_op jit(solution)/shard_map/ppermute | solution.py:240
  53.6 0.9 %add_add_fusion = f32[128,256]{1,0:T(8,128)S(1)} fusion(f32[128,256]{1,0:T(8,128)S(1)} %collective-permute-done.4, f32[128,256]{1,0:T(8,128)S(1)} %collective-permute-done.3, f32[128,256]{1,0:T(8,128)} %get-tuple-element.29, f32[128,256]{1,0:T(8,128)S(1)} %add.21), kind=kLoop, calls=%fused_computation | loop fusion | flops 98304 | bytes 655360 | tf_op jit(solution)/shard_map/add | solution.py:306
  54.5 2.1 %collective-permute-start.5 = (f32[128,256]{1,0:T(8,128)S(1)}, f32[128,256]{1,0:T(8,128)S(1)}, u32[]{:S(2)}, u32[]{:S(2)}) collective-permute-start(f32[128,256]{1,0:T(8,128)S(1)} %add_add_fusion), channel_id=1, source_target_pairs={{0,2},{1,3},{2,0},{3,1},{4,6},{5,7},{6,4},{7,5},{8,10},{9,11},{10,... | collective-permute-start | bytes 393224 | tf_op jit(solution)/shard_map/ppermute | solution.py:240
  56.6 3.8 %collective-permute-done.5 = f32[128,256]{1,0:T(8,128)S(1)} collective-permute-done((f32[128,256]{1,0:T(8,128)S(1)}, f32[128,256]{1,0:T(8,128)S(1)}, u32[]{:S(2)}, u32[]{:S(2)}) %collective-permute-start.5) | collective-permute-done | bytes 131104 | tf_op jit(solution)/shard_map/ppermute | solution.py:240
  60.4 1.9 %collective-permute-start.6 = (f32[128,256]{1,0:T(8,128)S(1)}, f32[128,256]{1,0:T(8,128)S(1)}, u32[]{:S(2)}, u32[]{:S(2)}) collective-permute-start(f32[128,256]{1,0:T(8,128)S(1)} %add.25), channel_id=1, source_target_pairs={{0,4},{1,5},{2,6},{3,7},{4,0},{5,1},{6,2},{7,3},{8,12},{9,13},{10,... | collective-permute-start | bytes 393224 | tf_op jit(solution)/shard_map/ppermute | solution.py:240
  62.3 3.1 %collective-permute-done.6 = f32[128,256]{1,0:T(8,128)S(1)} collective-permute-done((f32[128,256]{1,0:T(8,128)S(1)}, f32[128,256]{1,0:T(8,128)S(1)}, u32[]{:S(2)}, u32[]{:S(2)}) %collective-permute-start.6) | collective-permute-done | bytes 131104 | tf_op jit(solution)/shard_map/ppermute | solution.py:240
  65.5 3.9 %collective-permute-start.7 = (f32[128,256]{1,0:T(8,128)S(1)}, f32[128,256]{1,0:T(8,128)S(1)}, u32[]{:S(2)}, u32[]{:S(2)}) collective-permute-start(f32[128,256]{1,0:T(8,128)S(1)} %add.26), channel_id=1, source_target_pairs={{0,12},{1,13},{2,14},{3,15},{4,8},{5,9},{6,10},{7,11},{8,4},{9,5},... | collective-permute-start | bytes 393224 | tf_op jit(solution)/shard_map/ppermute | solution.py:240
  69.4 3.1 %collective-permute-done.7 = f32[128,256]{1,0:T(8,128)S(1)} collective-permute-done((f32[128,256]{1,0:T(8,128)S(1)}, f32[128,256]{1,0:T(8,128)S(1)}, u32[]{:S(2)}, u32[]{:S(2)}) %collective-permute-start.7) | collective-permute-done | bytes 131104 | tf_op jit(solution)/shard_map/ppermute | solution.py:240
  72.5 0.1 collective-permute-start.8
  72.5 3.7 %combine_leaf.1 = (f32[512,512]{1,0:T(8,128)}, f32[64,512]{1,0:T(8,128)}) custom-call(f32[256,576]{1,0:T(8,128)} %get-tuple-element.34.leaf_ref, f32[768,512]{1,0:T(8,128)} %get-tuple-element.27.after_ref.table_ref), custom_call_target="tpu_custom_call" | custom-call | flops 805306368 | bytes 2097152 | tf_op jit(solution)/shard_map/combine_leaf/pallas_call | solution.py:307
  76.2 2.9 %combine_region.1 = (f32[256,512]{1,0:T(8,128)}, f32[64,512]{1,0:T(8,128)}) custom-call(f32[256,320]{1,0:T(8,128)} %get-tuple-element.33.region_ref, f32[512,512]{1,0:T(8,128)} %get-tuple-element.35.upper_ref, f32[64,512]{1,0:T(8,128)} %get-tuple-element.36.leaf_base_ref), custom_call_target="tpu_custom_call" | custom-call | flops 402653184 | bytes 2097152 | tf_op jit(solution)/shard_map/combine_region/pallas_call | solution.py:315
  79.1 0.0 collective-permute-done.8.other_ref
  79.1 10.7 %predict.1 = f32[64,512]{1,0:T(8,128)} custom-call(s32[1]{0:T(128)} %bitcast.half_ref, f32[128,256]{1,0:T(8,128)S(1)} %add.27.mine_ref, f32[128,256]{1,0:T(8,128)S(1)} %collective-permute-done.8.other_ref, f32[256,256]{1,0:T(8,128)} %prior_ref.5, f32[256,512]{1,0:T(8,128)} %get-tuple-element.37.slope_ref, f32[64,512]{1,0:T(8,128)} %get-tuple-element.38.base_ref), custom_call_target="tpu_custom_call" | custom-call | flops 805306368 | bytes 2097152 | tf_op jit(solution)/shard_map/predict/pallas_call | solution.py:327
  (3 shorter events, 0.1 us)
Async XLA Ops:
  17.8 8.3 %copy-start = (f32[128,384]{1,0:T(8,128)S(1)}, f32[128,384]{1,0:T(8,128)}, u32[]{:S(2)}) copy-start(f32[128,384]{1,0:T(8,128)} %get-tuple-element.22.own_ref) | copy-start | bytes 589828
  23.1 25.5 %collective-permute-start.1 = (f32[128,640]{1,0:T(8,128)}, f32[128,640]{1,0:T(8,128)S(1)}, u32[]{:S(2)}, u32[]{:S(2)}) collective-permute-start(f32[128,640]{1,0:T(8,128)} %get-tuple-element.28.own_ref), channel_id=1, source_target_pairs={{0,16},{16,0},{1,17},{17,1},{2,18},{18,2},{3,19},{19,3},{4,20},{20... | collective-permute-start | bytes 983048 | tf_op jit(solution)/shard_map/ppermute | solution.py:240
  26.1 13.0 %collective-permute-start = (f32[128,384]{1,0:T(8,128)S(1)}, f32[128,384]{1,0:T(8,128)S(1)}, u32[]{:S(2)}, u32[]{:S(2)}) collective-permute-start(f32[128,384]{1,0:T(8,128)S(1)} %copy-done), channel_id=1, source_target_pairs={{0,16},{16,0},{1,17},{17,1},{2,18},{18,2},{3,19},{19,3},{4,20},{20... | collective-permute-start | bytes 589832 | tf_op jit(solution)/shard_map/ppermute | solution.py:240
  26.2 1.6 %collective-permute-start.2 = (f32[128,256]{1,0:T(8,128)}, f32[128,256]{1,0:T(8,128)S(1)}, u32[]{:S(2)}, u32[]{:S(2)}) collective-permute-start(f32[128,256]{1,0:T(8,128)} %get-tuple-element.31), channel_id=1, source_target_pairs={{0,1},{1,0},{2,3},{3,2},{4,5},{5,4},{6,7},{7,6},{8,9},{9,8},{10,11... | collective-permute-start | bytes 393224 | tf_op jit(solution)/shard_map/ppermute | solution.py:240
  28.6 23.4 %collective-permute-start.3 = (f32[128,256]{1,0:T(8,128)S(1)}, f32[128,256]{1,0:T(8,128)S(1)}, u32[]{:S(2)}, u32[]{:S(2)}) collective-permute-start(f32[128,256]{1,0:T(8,128)S(1)} %add.21), channel_id=1, source_target_pairs={{0,16},{16,0},{1,17},{17,1},{2,18},{18,2},{3,19},{19,3},{4,20},{20... | collective-permute-start | bytes 393224 | tf_op jit(solution)/shard_map/ppermute | solution.py:240
  52.0 1.6 %collective-permute-start.4 = (f32[128,256]{1,0:T(8,128)}, f32[128,256]{1,0:T(8,128)S(1)}, u32[]{:S(2)}, u32[]{:S(2)}) collective-permute-start(f32[128,256]{1,0:T(8,128)} %get-tuple-element.32), channel_id=1, source_target_pairs={{0,1},{1,0},{2,3},{3,2},{4,5},{5,4},{6,7},{7,6},{8,9},{9,8},{10,11... | collective-permute-start | bytes 393224 | tf_op jit(solution)/shard_map/ppermute | solution.py:240
  54.5 5.9 %collective-permute-start.5 = (f32[128,256]{1,0:T(8,128)S(1)}, f32[128,256]{1,0:T(8,128)S(1)}, u32[]{:S(2)}, u32[]{:S(2)}) collective-permute-start(f32[128,256]{1,0:T(8,128)S(1)} %add_add_fusion), channel_id=1, source_target_pairs={{0,2},{1,3},{2,0},{3,1},{4,6},{5,7},{6,4},{7,5},{8,10},{9,11},{10,... | collective-permute-start | bytes 393224 | tf_op jit(solution)/shard_map/ppermute | solution.py:240
  60.4 5.0 %collective-permute-start.6 = (f32[128,256]{1,0:T(8,128)S(1)}, f32[128,256]{1,0:T(8,128)S(1)}, u32[]{:S(2)}, u32[]{:S(2)}) collective-permute-start(f32[128,256]{1,0:T(8,128)S(1)} %add.25), channel_id=1, source_target_pairs={{0,4},{1,5},{2,6},{3,7},{4,0},{5,1},{6,2},{7,3},{8,12},{9,13},{10,... | collective-permute-start | bytes 393224 | tf_op jit(solution)/shard_map/ppermute | solution.py:240
  65.5 7.0 %collective-permute-start.7 = (f32[128,256]{1,0:T(8,128)S(1)}, f32[128,256]{1,0:T(8,128)S(1)}, u32[]{:S(2)}, u32[]{:S(2)}) collective-permute-start(f32[128,256]{1,0:T(8,128)S(1)} %add.26), channel_id=1, source_target_pairs={{0,12},{1,13},{2,14},{3,15},{4,8},{5,9},{6,10},{7,11},{8,4},{9,5},... | collective-permute-start | bytes 393224 | tf_op jit(solution)/shard_map/ppermute | solution.py:240
  72.5 6.6 %collective-permute-start.8 = (f32[128,256]{1,0:T(8,128)S(1)}, f32[128,256]{1,0:T(8,128)S(1)}, u32[]{:S(2)}, u32[]{:S(2)}) collective-permute-start(f32[128,256]{1,0:T(8,128)S(1)} %add.27.mine_ref), channel_id=1, source_target_pairs={{0,1},{1,0},{2,3},{3,2},{4,5},{5,4},{6,7},{7,6},{8,9},{9,8},{10,11... | collective-permute-start | bytes 393224 | tf_op jit(solution)/shard_map/ppermute | solution.py:240
